TPU v7x, 32 devices: a whole 2x2x4 slice. The times are simulated.
32 devices in a mesh: band: 8 (over z, x), ga: 4 (over y, core).
Axes of the slice: x: 2, y: 2, z: 4, core: 2. Of those that a mesh axis runs over, the one named last changes fastest.
Arguments:
- elements: bfloat16 [2, 768, 2048], P(None, 'band', 'ga'), may hold values from -0.75 to 0.75
- screened: bfloat16 [2, 2, 2048, 2048], P(None, None, 'ga'), may hold values from -0.09375 to 0.09375
- energies: float32 [768], replicated, may hold values from -3 to 3
- freq_points: float32 [2], replicated, may hold values from -3 to 3
- freq_weights: float32 [2], replicated, may hold values from 0.5 to 2
- band_of_slot: int32 [768], replicated, may hold values from 0 to 767, each once
Outputs:
- sigma: float32 [2, 768, 768], P(None, 'band', 'ga')
Inputs may be any that keep to these rules, and one draw needn't show every extreme that they name: `band_of_slot`: each of 0 to 767 stands once.
All inputs are finite; a program needn't handle non-finite values.
Results may differ from a plain program's by a relative error of at most 0.0042.
Values may be sent and summed in bfloat16 or wider, within the bound.
No kernel may reach another device: no remote copies, remote signals or barrier semaphores. Data moves between devices by JAX's collectives and lax.ppermute only.
A program may use at most 128 MiB of HBM per device.

v0:
```python
import jax
import jax.numpy as jnp
from jax import lax
from jax.sharding import PartitionSpec as P


BOTH = ("band", "ga")


def build(B, A):
    R = B // A

    def move(value, step):
        pairs = []
        for row in range(A):
            for r in range(R):
                for a in range(A):
                    to = step(row, r, a)
                    if to is not None:
                        pairs.append(((row * R + r) * A + a, (to[0] * R + to[1]) * A + to[2]))
        return lax.ppermute(value, BOTH, pairs)

    def swap(offset):
        return lambda row, r, a: (row ^ offset, r, a)

    def transpose(row, r, a):
        return (a, r, row)

    def flip(bit):
        return lambda row, r, a: (row, r, a ^ bit)

    def turn(offset):
        return lambda row, r, a: (row, (r - offset) % R, a)

    def on_device(elements, screened, energies, freq_points, freq_weights, band_of_slot):
        bands = elements.shape[1]
        band = lax.axis_index("band")
        row, r = band // R, band % R
        a = lax.axis_index("ga")

        high = A // 2
        across = move(elements, flip(high))
        beside = [move(elements, turn(o)) for o in range(1, R)]
        at = [elements]
        for o in range(1, A):
            at.append(move(elements, swap(o)))
        both = [
            jnp.stack([move(piece[0], flip(high)), move(across[1], turn(o))])
            for o, piece in zip(range(1, R), beside)
        ]
        mine = jnp.concatenate([elements] + beside, axis=1)
        far = jnp.concatenate([across] + both, axis=1)
        known = {0: mine, high: far}
        bit = high // 2
        while bit:
            for j in list(known):
                known[j | bit] = move(known[j], flip(bit))
            bit //= 2
        relative = jnp.stack([known[j] for j in range(A)])
        piece = jnp.concatenate(
            [lax.dynamic_index_in_dim(relative, j ^ a, 0, keepdims=False) for j in range(A)], axis=2
        )
        sides = jnp.stack([jnp.stack([piece[0], -piece[1]]), jnp.stack([piece[1], piece[0]])])
        applied = jnp.einsum(
            "dcmk,wcgk->wdmg", sides, screened, preferred_element_type=jnp.float32
        ).astype(jnp.bfloat16)

        at = jnp.stack(at)
        turned = [lax.dynamic_index_in_dim(at, row ^ a ^ j, 0, keepdims=False) for j in range(A)]

        band_of_slot, _ = lax.optimization_barrier((band_of_slot, far))
        slot_energy = jnp.take(energies, band_of_slot)
        offset = slot_energy[None, :] - freq_points[:, None]
        screen = freq_weights[:, None] / (1.0 + 4.0 * offset * offset)

        def screen_of(row_at, r_at):
            return lax.dynamic_slice_in_dim(screen, (row_at * R + r_at) * bands, bands, 1)

        right = jnp.concatenate([screen_of(row, (r + o) % R) for o in range(R)], axis=1)
        parts = {}
        for j in reversed(range(A)):
            block = turned[j]
            left = jnp.stack([block, jnp.stack([-block[1], block[0]])])
            pairs = jnp.einsum(
                "dcnk,wcmk->wdnm", left, applied, preferred_element_type=jnp.float32
            )
            factor = 0.5 * (screen_of(a ^ j, r)[:, :, None] + right[:, None, :])
            parts[j] = jnp.sum(pairs * factor[:, None], axis=0)
        bit = 1
        while bit < A:
            wire = jnp.float32 if bit < high else jnp.bfloat16
            kept = [j for j in parts if not j & bit]
            sent = jnp.stack([parts[j | bit].astype(wire) for j in kept])
            got = move(sent, flip(bit)).astype(jnp.float32)
            parts = {j: parts[j] + got[i] for i, j in enumerate(kept)}
            bit *= 2
        total = move(parts[0].astype(jnp.bfloat16), transpose).astype(jnp.float32)
        cut = jnp.split(total, R, axis=2)
        if R == 1:
            return total
        cut = jnp.stack(cut)
        return jnp.concatenate(
            [lax.dynamic_index_in_dim(cut, (j - r) % R, 0, keepdims=False) for j in range(R)], axis=2
        )

    return on_device


def solution(mesh):
    placed = (P(None, "band", "ga"), P(None, None, "ga", None), P(), P(), P(), P())
    A = mesh.shape["ga"]
    body = build(mesh.shape["band"], A)

    return jax.shard_map(
        body, mesh=mesh, in_specs=placed, out_specs=P(None, "band", "ga"), check_vma=False
    )
```

profile of v0, /device:TPU:4, one launch (start us, length us, event | category | flops | bytes accessed | tf_op | source)
XLA Modules:
  0.0 53.4 jit_solution(4874783555094463956)
XLA Ops:
  0.0 0.0 collective-permute-start.2
  0.0 2.0 %collective-permute-start = (bf16[2,96,512]{2,1,0:T(8,128)(2,1)}, bf16[2,96,512]{2,1,0:T(8,128)(2,1)S(1)}, u32[]{:S(2)}, u32[]{:S(2)}) collective-permute-start(bf16[2,96,512]{2,1,0:T(8,128)(2,1)} %param.6), channel_id=1, source_target_pairs={{0,4},{1,5},{2,6},{3,7},{4,0},{5,1},{6,2},{7,3},{8,12},{9,13},{10,... | collective-permute-start | bytes 589832 | tf_op jit(solution)/shard_map/ppermute | solution.py:21
  2.0 3.6 %collective-permute-start.8 = (bf16[2,96,512]{2,1,0:T(8,128)(2,1)}, bf16[2,96,512]{2,1,0:T(8,128)(2,1)S(1)}, u32[]{:S(2)}, u32[]{:S(2)}) collective-permute-start(bf16[2,96,512]{2,1,0:T(8,128)(2,1)} %param.6), channel_id=1, source_target_pairs={{0,24},{1,25},{2,26},{3,27},{4,28},{5,29},{6,30},{7,31},{8,16},{9,... | collective-permute-start | bytes 589832 | tf_op jit(solution)/shard_map/ppermute | solution.py:21
  5.6 0.8 %collective-permute-start.6 = (bf16[2,96,512]{2,1,0:T(8,128)(2,1)}, bf16[2,96,512]{2,1,0:T(8,128)(2,1)S(1)}, u32[]{:S(2)}, u32[]{:S(2)}) collective-permute-start(bf16[2,96,512]{2,1,0:T(8,128)(2,1)} %param.6), channel_id=1, source_target_pairs={{0,8},{1,9},{2,10},{3,11},{4,12},{5,13},{6,14},{7,15},{8,0},{9,1},... | collective-permute-start | bytes 589832 | tf_op jit(solution)/shard_map/ppermute | solution.py:21
  6.4 1.0 %constant_dynamic-update-slice_fusion.1 = bf16[2,192,512]{2,1,0:T(8,128)(2,1)S(1)} fusion(bf16[2,96,512]{2,1,0:T(8,128)(2,1)} %param.6), kind=kLoop, calls=%fused_computation.100 | loop fusion | bytes 393216
  7.4 1.0 %collective-permute-start.4 = (bf16[96,512]{1,0:T(8,128)(2,1)S(1)}, bf16[96,512]{1,0:T(8,128)(2,1)S(1)}, u32[]{:S(2)}, u32[]{:S(2)}) collective-permute-start(bf16[96,512]{1,0:T(8,128)(2,1)S(1)} %slice_bitcast_fusion.3), channel_id=1, source_target_pairs={{0,4},{1,5},{2,6},{3,7},{4,0},{5,1},{6,2},{7,3},{8,12},{9,13},{10,... | collective-permute-start | bytes 294920 | tf_op jit(solution)/shard_map/ppermute | solution.py:21
  8.4 0.0 collective-permute-done
  8.4 1.2 %collective-permute-start.3 = (bf16[96,512]{1,0:T(8,128)(2,1)S(1)}, bf16[96,512]{1,0:T(8,128)(2,1)S(1)}, u32[]{:S(2)}, u32[]{:S(2)}) collective-permute-start(bf16[96,512]{1,0:T(8,128)(2,1)S(1)} %slice_bitcast_fusion.4), channel_id=1, source_target_pairs={{0,2},{1,3},{2,0},{3,1},{4,6},{5,7},{6,4},{7,5},{8,10},{9,11},{10,... | collective-permute-start | bytes 294920 | tf_op jit(solution)/shard_map/ppermute | solution.py:21
  9.6 2.2 %collective-permute-done.8 = bf16[2,96,512]{2,1,0:T(8,128)(2,1)S(1)} collective-permute-done((bf16[2,96,512]{2,1,0:T(8,128)(2,1)}, bf16[2,96,512]{2,1,0:T(8,128)(2,1)S(1)}, u32[]{:S(2)}, u32[]{:S(2)}) %collective-permute-start.8) | collective-permute-done | bytes 196640 | tf_op jit(solution)/shard_map/ppermute | solution.py:21
  11.8 10.1 %collective-permute-done.7 = bf16[2,96,512]{2,1,0:T(8,128)(2,1)S(1)} collective-permute-done((bf16[2,96,512]{2,1,0:T(8,128)(2,1)}, bf16[2,96,512]{2,1,0:T(8,128)(2,1)S(1)}, u32[]{:S(2)}, u32[]{:S(2)}) %collective-permute-start.7) | collective-permute-done | bytes 196640 | tf_op jit(solution)/shard_map/ppermute | solution.py:21
  21.9 1.0 %pad_maximum_fusion.2 = bf16[4,2,96,512]{3,2,1,0:T(8,128)(2,1)S(1)} fusion(bf16[1,2,96,512]{3,2,1,0:T(8,128)(2,1)S(1)} %bitcast.154, bf16[1,2,96,512]{3,2,1,0:T(8,128)(2,1)S(1)} %bitcast.155, bf16[1,2,96,512]{3,2,1,0:T(8,128)(2,1)S(1)} %bitcast.156, bf16[1,2,96,512]{3,2,1,0:T(8,128)(2,1)} %bitcast.149), kind=kLoop, calls=%fused_computation.24 | loop fusion | flops 1179648 | bytes 1572864 | tf_op jit(solution)/shard_map/stack | solution.py:68
  23.0 0.1 constant_dynamic-slice_fusion.1
  23.1 0.1 fusion.35
  23.1 0.0 copy-start.2
  23.1 0.7 %maximum_bitcast_fusion.17 = (bf16[1,2,96,512]{3,2,1,0:T(8,128)(2,1)S(1)}, bf16[1,2,96,512]{3,2,1,0:T(8,128)(2,1)}) fusion(bf16[1,96,512]{2,1,0:T(8,128)(2,1)S(1)} %get-tuple-element.22, bf16[1,96,512]{2,1,0:T(8,128)(2,1)S(1)} %get-tuple-element.23, bf16[1,96,512]{2,1,0:T(8,128)(2,1)S(1)} %get-tuple-element.20, bf16[1,96,512]{2,1,0:T(8,128)(2,1)S(1)} %get-tuple-element.21), kind=kLoop, calls=%fused_computation.58 | loop fusion | flops 196608 | bytes 786432 | tf_op jit(solution)/shard_map/stack | solution.py:83
  23.9 0.1 fusion.46
  24.0 0.1 collective-permute-start.5
  24.1 0.0 copy-start.3
  24.1 0.0 copy-start.4
  24.1 3.2 %gather_fusion = f32[768]{0:T(1024)S(1)} fusion(f32[768]{0:T(1024)S(1)} %copy-done, s32[1024]{0:T(1024)S(1)} %pad_clamp_fusion), kind=kCustom, calls=%fused_computation | custom fusion | bytes 9216 | tf_op jit(solution)/shard_map/jit(_take)/gather | solution.py:72
  27.3 0.1 fusion.40
  27.4 0.1 constant_dynamic-slice_fusion
  27.5 0.1 pad_maximum_fusion.5
  27.6 0.1 add_multiply_fusion
  27.8 0.2 pad_maximum_fusion
  28.0 0.0 slice-start
  28.0 0.2 dynamic-slice_bitcast_fusion.3
  28.2 0.2 pad_maximum_fusion.1
  28.4 0.0 slice-start.1
  28.4 0.2 slice_negate_fusion
  28.6 0.3 maximum_bitcast_fusion.2
  28.8 1.3 %slice-done = s8[4194304]{0:T(1024)(128)(4,1)S(1)} async-done(((s8[8388608]{0:T(1024)(128)(4,1)}), s8[4194304]{0:T(1024)(128)(4,1)S(1)}, s32[]{:S(2)}) %slice-start) | async-done | bytes 4194328
  30.2 1.4 %slice-done.1 = s8[4194304]{0:T(1024)(128)(4,1)S(1)} async-done(((s8[8388608]{0:T(1024)(128)(4,1)}), s8[4194304]{0:T(1024)(128)(4,1)S(1)}, s32[]{:S(2)}) %slice-start.1) | async-done | bytes 4194328
  31.5 3.4 %fusion.6 = bf16[2,2,192,512,1]{3,2,0,1,4:T(8,128)(2,1)S(1)} fusion(bf16[2,2,512,2048]{3,2,1,0:T(8,128)(2,1)S(1)} %bitcast.162, bf16[1,2,192,2048]{3,2,1,0:T(8,128)(2,1)S(1)} %get-tuple-element.27, bf16[1,2,192,2048]{3,2,1,0:T(8,128)(2,1)S(1)} %get-tuple-element.26), kind=kOutput, calls=%fused_computation.11 | convolution fusion | flops 3227910144 | bytes 12320768 | tf_op jit(solution)/shard_map/dcmk,wcgk->wdmg/dot_general | solution.py:64
  35.0 0.4 fusion.14
  35.4 0.4 fusion.15
  35.9 0.5 %collective-permute-start.9 = (f32[2,2,96,192]{2,3,1,0:T(8,128)S(1)}, f32[2,2,96,192]{2,3,1,0:T(8,128)S(1)}, u32[]{:S(2)}, u32[]{:S(2)}) collective-permute-start(f32[2,2,96,192]{2,3,1,0:T(8,128)S(1)} %pad_maximum_fusion.3), channel_id=1, source_target_pairs={{0,1},{1,0},{2,3},{3,2},{4,5},{5,4},{6,7},{7,6},{8,9},{9,8},{10,11... | collective-permute-start | bytes 884744 | tf_op jit(solution)/shard_map/ppermute | solution.py:21
  36.4 0.4 fusion.13
  36.8 0.9 %collective-permute-done.9 = f32[2,2,96,192]{2,3,1,0:T(8,128)S(1)} collective-permute-done((f32[2,2,96,192]{2,3,1,0:T(8,128)S(1)}, f32[2,2,96,192]{2,3,1,0:T(8,128)S(1)}, u32[]{:S(2)}, u32[]{:S(2)}) %collective-permute-start.9) | collective-permute-done | bytes 294944 | tf_op jit(solution)/shard_map/ppermute | solution.py:21
  37.8 1.6 %collective-permute-start.10 = (bf16[1,2,96,192]{2,3,1,0:T(8,128)(2,1)S(1)}, bf16[1,2,96,192]{2,3,1,0:T(8,128)(2,1)S(1)}, u32[]{:S(2)}, u32[]{:S(2)}) collective-permute-start(bf16[1,2,96,192]{2,3,1,0:T(8,128)(2,1)S(1)} %fusion.29), channel_id=1, source_target_pairs={{0,2},{1,3},{2,0},{3,1},{4,6},{5,7},{6,4},{7,5},{8,10},{9,11},{10,... | collective-permute-start | bytes 221192 | tf_op jit(solution)/shard_map/ppermute | solution.py:21
  39.4 0.4 fusion.16
  39.8 3.2 %collective-permute-done.10 = bf16[1,2,96,192]{2,3,1,0:T(8,128)(2,1)S(1)} collective-permute-done((bf16[1,2,96,192]{2,3,1,0:T(8,128)(2,1)S(1)}, bf16[1,2,96,192]{2,3,1,0:T(8,128)(2,1)S(1)}, u32[]{:S(2)}, u32[]{:S(2)}) %collective-permute-start.10) | collective-permute-done | bytes 73760 | tf_op jit(solution)/shard_map/ppermute | solution.py:21
  42.9 2.5 %collective-permute-start.11 = (bf16[2,96,192]{1,2,0:T(8,128)(2,1)S(1)}, bf16[2,96,192]{1,2,0:T(8,128)(2,1)S(1)}, u32[]{:S(2)}, u32[]{:S(2)}) collective-permute-start(bf16[2,96,192]{1,2,0:T(8,128)(2,1)S(1)} %fusion.32), channel_id=1, source_target_pairs={{0,0},{1,8},{2,16},{3,24},{4,4},{5,12},{6,20},{7,28},{8,1},{9,9},{... | collective-permute-start | bytes 221192 | tf_op jit(solution)/shard_map/ppermute | solution.py:21
  45.5 6.8 %collective-permute-done.11 = bf16[2,96,192]{1,2,0:T(8,128)(2,1)S(1)} collective-permute-done((bf16[2,96,192]{1,2,0:T(8,128)(2,1)S(1)}, bf16[2,96,192]{1,2,0:T(8,128)(2,1)S(1)}, u32[]{:S(2)}, u32[]{:S(2)}) %collective-permute-start.11) | collective-permute-done | bytes 73760 | tf_op jit(solution)/shard_map/ppermute | solution.py:21
  52.4 0.1 fusion.34
  52.4 0.1 copy.24
  52.5 0.1 copy.23
  52.6 0.8 %pad_maximum_fusion.4 = f32[2,96,192]{2,1,0:T(8,128)} fusion(f32[2,96,96]{2,1,0:T(8,128)S(1)} %bitcast.152, f32[2,96,96]{2,1,0:T(8,128)S(1)} %bitcast.153), kind=kLoop, calls=%fused_computation.61 | loop fusion | flops 36864 | bytes 294912 | tf_op jit(solution)/shard_map/concatenate | solution.py:102
  (29 shorter events, 0.2 us)
Async XLA Ops:
  0.0 24.1 %copy-start = (f32[768]{0:T(1024)S(1)}, f32[768]{0:T(1024)}, u32[]{:S(2)}) copy-start(f32[768]{0:T(1024)} %param.8) | copy-start | bytes 9220
  0.0 7.4 %collective-permute-start.2 = (bf16[2,96,512]{2,1,0:T(8,128)(2,1)}, bf16[2,96,512]{2,1,0:T(8,128)(2,1)S(1)}, u32[]{:S(2)}, u32[]{:S(2)}) collective-permute-start(bf16[2,96,512]{2,1,0:T(8,128)(2,1)} %param.6), channel_id=1, source_target_pairs={{0,2},{1,3},{2,0},{3,1},{4,6},{5,7},{6,4},{7,5},{8,10},{9,11},{10,... | collective-permute-start | bytes 589832 | tf_op jit(solution)/shard_map/ppermute | solution.py:21
  0.0 8.4 %collective-permute-start = (bf16[2,96,512]{2,1,0:T(8,128)(2,1)}, bf16[2,96,512]{2,1,0:T(8,128)(2,1)S(1)}, u32[]{:S(2)}, u32[]{:S(2)}) collective-permute-start(bf16[2,96,512]{2,1,0:T(8,128)(2,1)} %param.6), channel_id=1, source_target_pairs={{0,4},{1,5},{2,6},{3,7},{4,0},{5,1},{6,2},{7,3},{8,12},{9,13},{10,... | collective-permute-start | bytes 589832 | tf_op jit(solution)/shard_map/ppermute | solution.py:21
  2.0 9.8 %collective-permute-start.8 = (bf16[2,96,512]{2,1,0:T(8,128)(2,1)}, bf16[2,96,512]{2,1,0:T(8,128)(2,1)S(1)}, u32[]{:S(2)}, u32[]{:S(2)}) collective-permute-start(bf16[2,96,512]{2,1,0:T(8,128)(2,1)} %param.6), channel_id=1, source_target_pairs={{0,24},{1,25},{2,26},{3,27},{4,28},{5,29},{6,30},{7,31},{8,16},{9,... | collective-permute-start | bytes 589832 | tf_op jit(solution)/shard_map/ppermute | solution.py:21
  5.6 16.3 %collective-permute-start.7 = (bf16[2,96,512]{2,1,0:T(8,128)(2,1)}, bf16[2,96,512]{2,1,0:T(8,128)(2,1)S(1)}, u32[]{:S(2)}, u32[]{:S(2)}) collective-permute-start(bf16[2,96,512]{2,1,0:T(8,128)(2,1)} %param.6), channel_id=1, source_target_pairs={{0,16},{1,17},{2,18},{3,19},{4,20},{5,21},{6,22},{7,23},{8,24},{9,... | collective-permute-start | bytes 589832 | tf_op jit(solution)/shard_map/ppermute | solution.py:21
  5.6 16.3 %collective-permute-start.6 = (bf16[2,96,512]{2,1,0:T(8,128)(2,1)}, bf16[2,96,512]{2,1,0:T(8,128)(2,1)S(1)}, u32[]{:S(2)}, u32[]{:S(2)}) collective-permute-start(bf16[2,96,512]{2,1,0:T(8,128)(2,1)} %param.6), channel_id=1, source_target_pairs={{0,8},{1,9},{2,10},{3,11},{4,12},{5,13},{6,14},{7,15},{8,0},{9,1},... | collective-permute-start | bytes 589832 | tf_op jit(solution)/shard_map/ppermute | solution.py:21
  7.4 16.5 %collective-permute-start.4 = (bf16[96,512]{1,0:T(8,128)(2,1)S(1)}, bf16[96,512]{1,0:T(8,128)(2,1)S(1)}, u32[]{:S(2)}, u32[]{:S(2)}) collective-permute-start(bf16[96,512]{1,0:T(8,128)(2,1)S(1)} %slice_bitcast_fusion.3), channel_id=1, source_target_pairs={{0,4},{1,5},{2,6},{3,7},{4,0},{5,1},{6,2},{7,3},{8,12},{9,13},{10,... | collective-permute-start | bytes 294920 | tf_op jit(solution)/shard_map/ppermute | solution.py:21
  8.4 15.5 %collective-permute-start.3 = (bf16[96,512]{1,0:T(8,128)(2,1)S(1)}, bf16[96,512]{1,0:T(8,128)(2,1)S(1)}, u32[]{:S(2)}, u32[]{:S(2)}) collective-permute-start(bf16[96,512]{1,0:T(8,128)(2,1)S(1)} %slice_bitcast_fusion.4), channel_id=1, source_target_pairs={{0,2},{1,3},{2,0},{3,1},{4,6},{5,7},{6,4},{7,5},{8,10},{9,11},{10,... | collective-permute-start | bytes 294920 | tf_op jit(solution)/shard_map/ppermute | solution.py:21
  11.8 15.9 %collective-permute-start.1 = (bf16[2,192,512]{2,1,0:T(8,128)(2,1)S(1)}, bf16[2,192,512]{2,1,0:T(8,128)(2,1)S(1)}, u32[]{:S(2)}, u32[]{:S(2)}) collective-permute-start(bf16[2,192,512]{2,1,0:T(8,128)(2,1)S(1)} %constant_dynamic-update-slice_fusion), channel_id=1, source_target_pairs={{0,1},{1,0},{2,3},{3,2},{4,5},{5,4},{6,7},{7,6},{8,9},{9,8},{10,11... | collective-permute-start | bytes 1179656 | tf_op jit(solution)/shard_map/ppermute | solution.py:21
  23.1 0.9 %copy-start.2 = (s32[768]{0:T(1024)S(1)}, s32[768]{0:T(1024)}, u32[]{:S(2)}) copy-start(s32[768]{0:T(1024)} %param.11) | copy-start | bytes 9220
  24.0 3.8 %collective-permute-start.5 = (bf16[2,192,512]{2,1,0:T(8,128)(2,1)S(1)}, bf16[2,192,512]{2,1,0:T(8,128)(2,1)S(1)}, u32[]{:S(2)}, u32[]{:S(2)}) collective-permute-start(bf16[2,192,512]{2,1,0:T(8,128)(2,1)S(1)} %get-tuple-element.29), channel_id=1, source_target_pairs={{0,1},{1,0},{2,3},{3,2},{4,5},{5,4},{6,7},{7,6},{8,9},{9,8},{10,11... | collective-permute-start | bytes 1179656 | tf_op jit(solution)/shard_map/ppermute | solution.py:21
  24.1 3.2 %copy-start.3 = (f32[2]{0:T(128)S(1)}, f32[2]{0:T(128)}, u32[]{:S(2)}) copy-start(f32[2]{0:T(128)} %param.10) | copy-start | bytes 28
  24.1 3.2 %copy-start.4 = (f32[2]{0:T(128)S(1)}, f32[2]{0:T(128)}, u32[]{:S(2)}) copy-start(f32[2]{0:T(128)} %param.9) | copy-start | bytes 28
  28.0 2.2 %slice-start = ((s8[8388608]{0:T(1024)(128)(4,1)}), s8[4194304]{0:T(1024)(128)(4,1)S(1)}, s32[]{:S(2)}) async-start(s8[8388608]{0:T(1024)(128)(4,1)} %bitcast.161), calls=%async_computation | async-start | bytes 8388608
  28.4 3.2 %slice-start.1 = ((s8[8388608]{0:T(1024)(128)(4,1)}), s8[4194304]{0:T(1024)(128)(4,1)S(1)}, s32[]{:S(2)}) async-start(s8[8388608]{0:T(1024)(128)(4,1)} %bitcast.161), calls=%async_computation.1 | async-start | bytes 8388608
  31.5 3.5 %copy-start.1 = (bf16[1,2,96,512]{3,2,1,0:T(8,128)(2,1)S(1)}, bf16[1,2,96,512]{3,2,1,0:T(8,128)(2,1)}, u32[]{:S(2)}) copy-start(bf16[1,2,96,512]{3,2,1,0:T(8,128)(2,1)} %get-tuple-element.45) | copy-start | bytes 589828
  35.9 1.9 %collective-permute-start.9 = (f32[2,2,96,192]{2,3,1,0:T(8,128)S(1)}, f32[2,2,96,192]{2,3,1,0:T(8,128)S(1)}, u32[]{:S(2)}, u32[]{:S(2)}) collective-permute-start(f32[2,2,96,192]{2,3,1,0:T(8,128)S(1)} %pad_maximum_fusion.3), channel_id=1, source_target_pairs={{0,1},{1,0},{2,3},{3,2},{4,5},{5,4},{6,7},{7,6},{8,9},{9,8},{10,11... | collective-permute-start | bytes 884744 | tf_op jit(solution)/shard_map/ppermute | solution.py:21
  37.8 5.1 %collective-permute-start.10 = (bf16[1,2,96,192]{2,3,1,0:T(8,128)(2,1)S(1)}, bf16[1,2,96,192]{2,3,1,0:T(8,128)(2,1)S(1)}, u32[]{:S(2)}, u32[]{:S(2)}) collective-permute-start(bf16[1,2,96,192]{2,3,1,0:T(8,128)(2,1)S(1)} %fusion.29), channel_id=1, source_target_pairs={{0,2},{1,3},{2,0},{3,1},{4,6},{5,7},{6,4},{7,5},{8,10},{9,11},{10,... | collective-permute-start | bytes 221192 | tf_op jit(solution)/shard_map/ppermute | solution.py:21
  42.9 9.4 %collective-permute-start.11 = (bf16[2,96,192]{1,2,0:T(8,128)(2,1)S(1)}, bf16[2,96,192]{1,2,0:T(8,128)(2,1)S(1)}, u32[]{:S(2)}, u32[]{:S(2)}) collective-permute-start(bf16[2,96,192]{1,2,0:T(8,128)(2,1)S(1)} %fusion.32), channel_id=1, source_target_pairs={{0,0},{1,8},{2,16},{3,24},{4,4},{5,12},{6,20},{7,28},{8,1},{9,9},{... | collective-permute-start | bytes 221192 | tf_op jit(solution)/shard_map/ppermute | solution.py:21
where the time goes:
time: 53.6 us; the launch traced here: 53.4 us
  waiting for transfers between devices  23.2 us (43%)
  starting transfers between devices  13.3 us (25%)
  local copies, waits for them, and re-layouts  7.46 us (14%)
  matrix products  5.02 us (9%)
  other arithmetic  3.99 us (7%)
    ppermute x12, waiting for transfers between devices, move(): return lax.ppermute(value, BOTH, pairs)  23.2 us
    ppermute x12, starting transfers between devices, move(): return lax.ppermute(value, BOTH, pairs)  13.3 us
    unnamed x15, local copies, waits for them, and re-layouts  3.72 us
    dot_general x1, matrix products, on_device(): jnp.einsum('dcmk,wcgk->wdmg', sides, screened, preferred_element_type=jnp...  3.45 us
    gather x1, local copies, waits for them, and re-layouts, on_device(): slot_energy = jnp.take(energies, band_of_slot)  3.19 us
    dot_general x4, matrix products, on_device(): jnp.einsum('dcnk,wcmk->wdnm', left, applied, preferred_element_type=jnp.f...  1.57 us
  transfers between devices with their start and end apart: 12, of which 5 were waited for; matrix products, arithmetic and copies ran while one was open for 14% of the time, Pallas kernels for 0%

commit v1 on v0

--- a/solution.py
+++ b/solution.py
@@ -1,10 +1,65 @@
 import jax
 import jax.numpy as jnp
 from jax import lax
+from jax.experimental import pallas as pl
+from jax.experimental.pallas import tpu as pltpu
 from jax.sharding import PartitionSpec as P
 
 
 BOTH = ("band", "ga")
+
+
+def apply_screened(order, pieces, screened):
+    count = len(pieces)
+    _, m, k = pieces[0].shape
+    freqs, _, g, total = screened.shape
+    tile = min(g, 256)
+
+    def kernel(order_ref, *refs):
+        piece_refs, w_ref, out_ref = refs[:count], refs[count], refs[count + 1]
+        real, imag, minus = refs[count + 2:]
+
+        @pl.when((pl.program_id(0) == 0) & (pl.program_id(1) == 0))
+        def _():
+            for j in range(count):
+                columns = pl.ds(pl.multiple_of(order_ref[j] * k, k), k)
+                real[:, columns] = piece_refs[j][0]
+                imag[:, columns] = piece_refs[j][1]
+                minus[:, columns] = -piece_refs[j][1]
+
+        def dot(left, right):
+            return lax.dot_general(
+                left, right, (((1,), (1,)), ((), ())), preferred_element_type=jnp.float32
+            )
+
+        first = dot(real[...], w_ref[0, 0]) + dot(minus[...], w_ref[0, 1])
+        out_ref[0, 0] = first.astype(jnp.bfloat16)
+        second = dot(imag[...], w_ref[0, 0]) + dot(real[...], w_ref[0, 1])
+        out_ref[0, 1] = second.astype(jnp.bfloat16)
+
+    whole = pl.BlockSpec((2, m, k), lambda w, t, order_ref: (0, 0, 0))
+    return pl.pallas_call(
+        kernel,
+        grid_spec=pltpu.PrefetchScalarGridSpec(
+            num_scalar_prefetch=1,
+            grid=(freqs, g // tile),
+            in_specs=[whole] * count
+            + [pl.BlockSpec((1, 2, tile, total), lambda w, t, order_ref: (w, 0, t, 0))],
+            out_specs=pl.BlockSpec((1, 2, m, tile), lambda w, t, order_ref: (w, 0, 0, t)),
+            scratch_shapes=[pltpu.VMEM((m, total), jnp.bfloat16)] * 3,
+        ),
+        out_shape=jax.ShapeDtypeStruct((freqs, 2, m, g), jnp.bfloat16),
+        compiler_params=pltpu.CompilerParams(vmem_limit_bytes=40 * 2**20),
+        cost_estimate=pl.CostEstimate(
+            flops=8 * freqs * m * g * total,
+            bytes_accessed=2 * screened.size + 4 * freqs * m * g + 4 * m * total,
+            transcendentals=0,
+        ),
+    )(order, *pieces, screened)
+
+
+def small(R):
+    return R <= 4
 
 
 def build(B, A):
@@ -56,20 +111,28 @@
             for j in list(known):
                 known[j | bit] = move(known[j], flip(bit))
             bit //= 2
-        relative = jnp.stack([known[j] for j in range(A)])
-        piece = jnp.concatenate(
-            [lax.dynamic_index_in_dim(relative, j ^ a, 0, keepdims=False) for j in range(A)], axis=2
-        )
-        sides = jnp.stack([jnp.stack([piece[0], -piece[1]]), jnp.stack([piece[1], piece[0]])])
-        applied = jnp.einsum(
-            "dcmk,wcgk->wdmg", sides, screened, preferred_element_type=jnp.float32
-        ).astype(jnp.bfloat16)
+        if small(R):
+            order = jnp.stack([a ^ j for j in range(A)]).astype(jnp.int32)
+            applied = apply_screened(order, [known[j] for j in range(A)], screened)
+        else:
+            relative = jnp.stack([known[j] for j in range(A)])
+            piece = jnp.concatenate(
+                [lax.dynamic_index_in_dim(relative, j ^ a, 0, keepdims=False) for j in range(A)],
+                axis=2,
+            )
+            sides = jnp.stack([jnp.stack([piece[0], -piece[1]]), jnp.stack([piece[1], piece[0]])])
+            applied = jnp.einsum(
+                "dcmk,wcgk->wdmg", sides, screened, preferred_element_type=jnp.float32
+            ).astype(jnp.bfloat16)
 
         at = jnp.stack(at)
         turned = [lax.dynamic_index_in_dim(at, row ^ a ^ j, 0, keepdims=False) for j in range(A)]
 
-        band_of_slot, _ = lax.optimization_barrier((band_of_slot, far))
-        slot_energy = jnp.take(energies, band_of_slot)
+        if small(R):
+            hit = band_of_slot[None, :] == lax.iota(jnp.int32, energies.shape[0])[:, None]
+            slot_energy = jnp.sum(jnp.where(hit, energies[:, None], 0.0), axis=0)
+        else:
+            slot_energy = jnp.take(energies, band_of_slot)
         offset = slot_energy[None, :] - freq_points[:, None]
         screen = freq_weights[:, None] / (1.0 + 4.0 * offset * offset)
 

time: 53.6 us -> 51.4 us (0.959)
  Pallas kernels: 0 us -> 7.54 us
  local copies, waits for them, and re-layouts: 7.46 us -> 1.48 us
  matrix products: 5.02 us -> 1.57 us
  starting transfers between devices: 13.3 us -> 16.6 us
  waiting for transfers between devices: 23.2 us -> 20.3 us
  other arithmetic: 3.99 us -> 3.31 us
    pallas_call x0 -> x1, Pallas kernels: none -> 7.54 us  [apply_screened(): pl.pallas_call(kernel, grid_spec=pltpu.PrefetchScalarGridSpec(num_scalar_...]
    dot_general x1 -> x0, matrix products: 3.45 us -> none  [on_device(): jnp.einsum('dcmk,wcgk->wdmg', sides, screened, preferred_element_type=jnp...]
    ppermute x12, starting transfers between devices: 13.3 us -> 16.6 us  [move(): return lax.ppermute(value, BOTH, pairs)]
    gather x1 -> x0, local copies, waits for them, and re-layouts: 3.19 us -> none  [on_device(): slot_energy = jnp.take(energies, band_of_slot)]
    ppermute x12, waiting for transfers between devices: 23.2 us -> 20.3 us  [move(): return lax.ppermute(value, BOTH, pairs)]
    unnamed x15 -> x5, local copies, waits for them, and re-layouts: 3.72 us -> 1.1 us
    reduce_sum x0 -> x1, other arithmetic: none -> 1.05 us  [on_device(): slot_energy = jnp.sum(jnp.where(hit, energies[:, None], 0.0), axis=0)]
    another operation x1, other arithmetic: 1.03 us -> 0.1 us  [on_device(): at = jnp.stack(at)]
  transfers between devices with their start and end apart: 12 -> 12, of which waited for: 5 -> 6; matrix products, arithmetic and copies ran while one was open for 14% -> 9% of each run, Pallas kernels for 0% -> 0%
where the time goes in v1:
time: 51.4 us; the launch traced here: 51.2 us
  waiting for transfers between devices  20.3 us (39%)
  starting transfers between devices  16.6 us (32%)
  Pallas kernels  7.54 us (15%)
  other arithmetic  3.31 us (6%)
  matrix products  1.57 us (3%)
  local copies, waits for them, and re-layouts  1.48 us (3%)
    ppermute x12, waiting for transfers between devices, move(): return lax.ppermute(value, BOTH, pairs)  20.3 us
    ppermute x12, starting transfers between devices, move(): return lax.ppermute(value, BOTH, pairs)  16.6 us
    pallas_call x1, Pallas kernels, apply_screened(): pl.pallas_call(kernel, grid_spec=pltpu.PrefetchScalarGridSpec(num_scalar_...  7.54 us
    dot_general x4, matrix products, on_device(): jnp.einsum('dcnk,wcmk->wdnm', left, applied, preferred_element_type=jnp.f...  1.57 us
    unnamed x5, local copies, waits for them, and re-layouts  1.1 us
    reduce_sum x1, other arithmetic, on_device(): slot_energy = jnp.sum(jnp.where(hit, energies[:, None], 0.0), axis=0)  1.05 us
  transfers between devices with their start and end apart: 12, of which 6 were waited for; matrix products, arithmetic and copies ran while one was open for 9% of the time, Pallas kernels for 0%

profile of v1, /device:TPU:4, one launch (start us, length us, event | category | flops | bytes accessed | tf_op | source)
XLA Modules:
  0.0 51.2 jit_solution(7534016776604947359)
XLA Ops:
  0.0 0.0 copy-start.1
  0.0 1.5 %collective-permute-start = (bf16[2,96,512]{2,1,0:T(8,128)(2,1)}, bf16[2,96,512]{2,1,0:T(8,128)(2,1)S(1)}, u32[]{:S(2)}, u32[]{:S(2)}) collective-permute-start(bf16[2,96,512]{2,1,0:T(8,128)(2,1)} %param.6), channel_id=1, source_target_pairs={{0,4},{1,5},{2,6},{3,7},{4,0},{5,1},{6,2},{7,3},{8,12},{9,13},{10,... | collective-permute-start | bytes 589832 | tf_op jit(solution)/shard_map/ppermute | solution.py:76
  1.5 0.5 collective-permute-start.2
  2.0 3.6 %collective-permute-start.8 = (bf16[2,96,512]{2,1,0:T(8,128)(2,1)}, bf16[2,96,512]{2,1,0:T(8,128)(2,1)S(1)}, u32[]{:S(2)}, u32[]{:S(2)}) collective-permute-start(bf16[2,96,512]{2,1,0:T(8,128)(2,1)} %param.6), channel_id=1, source_target_pairs={{0,24},{1,25},{2,26},{3,27},{4,28},{5,29},{6,30},{7,31},{8,16},{9,... | collective-permute-start | bytes 589832 | tf_op jit(solution)/shard_map/ppermute | solution.py:76
  5.6 0.0 collective-permute-start.7
  5.6 0.8 %collective-permute-start.6 = (bf16[2,96,512]{2,1,0:T(8,128)(2,1)}, bf16[2,96,512]{2,1,0:T(8,128)(2,1)S(1)}, u32[]{:S(2)}, u32[]{:S(2)}) collective-permute-start(bf16[2,96,512]{2,1,0:T(8,128)(2,1)} %param.6), channel_id=1, source_target_pairs={{0,8},{1,9},{2,10},{3,11},{4,12},{5,13},{6,14},{7,15},{8,0},{9,1},... | collective-permute-start | bytes 589832 | tf_op jit(solution)/shard_map/ppermute | solution.py:76
  6.4 1.0 %select_reduce_fusion = f32[768]{0:T(1024)S(1)} fusion(f32[768]{0:T(1024)} %param.8, s32[768]{0:T(1024)} %param.11), kind=kLoop, calls=%fused_computation | loop fusion | flops 1768704 | bytes 9216 | tf_op jit(solution)/shard_map/reduce_sum | solution.py:133
  7.5 0.8 %fusion.31 = f32[2,768]{1,0:T(2,128)S(1)} fusion(f32[2]{0:T(128)} %param.10, f32[768]{0:T(1024)S(1)} %select_reduce_fusion, f32[2]{0:T(128)} %param.9), kind=kLoop, calls=%fused_computation.72 | loop fusion | flops 7680 | bytes 9232 | tf_op jit(solution)/shard_map/div | solution.py:137
  8.2 0.1 constant_dynamic-slice_fusion
  8.3 0.1 pad_maximum_fusion.3
  8.4 0.0 copy-start
  8.4 0.1 add_multiply_fusion
  8.6 1.1 %constant_dynamic-update-slice_fusion.1 = bf16[2,192,512]{2,1,0:T(8,128)(2,1)S(1)} fusion(bf16[2,96,512]{2,1,0:T(8,128)(2,1)} %param.6), kind=kLoop, calls=%fused_computation.74 | loop fusion | bytes 393216
  9.7 0.1 pad_add_fusion.order_ref
  9.7 0.0 collective-permute-done
  9.8 0.1 collective-permute-start.1
  9.8 0.0 collective-permute-done.2
  9.9 0.4 collective-permute-start.4
  10.3 1.6 %collective-permute-done.8 = bf16[2,96,512]{2,1,0:T(8,128)(2,1)S(1)} collective-permute-done((bf16[2,96,512]{2,1,0:T(8,128)(2,1)}, bf16[2,96,512]{2,1,0:T(8,128)(2,1)S(1)}, u32[]{:S(2)}, u32[]{:S(2)}) %collective-permute-start.8) | collective-permute-done | bytes 196640 | tf_op jit(solution)/shard_map/ppermute | solution.py:76
  11.8 1.5 %collective-permute-start.3 = (bf16[96,512]{1,0:T(8,128)(2,1)S(1)}, bf16[96,512]{1,0:T(8,128)(2,1)S(1)}, u32[]{:S(2)}, u32[]{:S(2)}) collective-permute-start(bf16[96,512]{1,0:T(8,128)(2,1)S(1)} %slice_bitcast_fusion.4), channel_id=1, source_target_pairs={{0,2},{1,3},{2,0},{3,1},{4,6},{5,7},{6,4},{7,5},{8,10},{9,11},{10,... | collective-permute-start | bytes 294920 | tf_op jit(solution)/shard_map/ppermute | solution.py:76
  13.4 8.6 %collective-permute-done.7 = bf16[2,96,512]{2,1,0:T(8,128)(2,1)S(1)} collective-permute-done((bf16[2,96,512]{2,1,0:T(8,128)(2,1)}, bf16[2,96,512]{2,1,0:T(8,128)(2,1)S(1)}, u32[]{:S(2)}, u32[]{:S(2)}) %collective-permute-start.7) | collective-permute-done | bytes 196640 | tf_op jit(solution)/shard_map/ppermute | solution.py:76
  21.9 0.0 collective-permute-done.6
  21.9 0.0 copy-done.1
  22.0 0.1 pad_maximum_fusion
  22.1 0.0 collective-permute-done.4
  22.1 0.0 collective-permute-done.3
  22.1 0.1 collective-permute-start.5
  22.2 0.1 fusion.26
  22.3 0.1 constant_dynamic-slice_fusion.1
  22.4 0.0 collective-permute-done.1.refs_1_
  22.4 1.5 %collective-permute-done.5.refs_3_ = bf16[2,192,512]{2,1,0:T(8,128)(2,1)S(1)} collective-permute-done((bf16[2,192,512]{2,1,0:T(8,128)(2,1)S(1)}, bf16[2,192,512]{2,1,0:T(8,128)(2,1)S(1)}, u32[]{:S(2)}, u32[]{:S(2)}) %collective-permute-start.5) | collective-permute-done | bytes 393248 | tf_op jit(solution)/shard_map/ppermute | solution.py:76
  23.9 0.0 copy-done
  23.9 7.5 %shard_map.64 = bf16[2,2,192,512]{3,2,1,0:T(8,128)(2,1)S(1)} custom-call(s32[4]{0:T(128)S(1)} %pad_add_fusion.order_ref, bf16[2,192,512]{2,1,0:T(8,128)(2,1)S(1)} %constant_dynamic-update-slice_fusion.refs_0_, bf16[2,192,512]{2,1,0:T(8,128)(2,1)S(1)} %collective-permute-done.1.refs_1_, bf16[2,192,512]{2,1,0:T(8,128)(2,1)S(1)} %maximum_maximum_fusion.refs_2_, ...), custom_call_target="tpu_custom_call" | custom-call | flops 3221225472 | bytes 10747904 | tf_op jit(solution)/shard_map/pallas_call | solution.py:41
  31.5 0.4 fusion.5
  31.9 0.4 fusion.6
  32.3 0.2 collective-permute-start.9
  32.5 0.4 fusion.4
  32.9 1.2 %collective-permute-done.9 = f32[2,2,96,192]{2,3,1,0:T(8,128)S(1)} collective-permute-done((f32[2,2,96,192]{2,3,1,0:T(8,128)S(1)}, f32[2,2,96,192]{2,3,1,0:T(8,128)S(1)}, u32[]{:S(2)}, u32[]{:S(2)}) %collective-permute-start.9) | collective-permute-done | bytes 294944 | tf_op jit(solution)/shard_map/ppermute | solution.py:76
  34.1 1.6 %collective-permute-start.10 = (bf16[1,2,96,192]{2,3,1,0:T(8,128)(2,1)S(1)}, bf16[1,2,96,192]{2,3,1,0:T(8,128)(2,1)S(1)}, u32[]{:S(2)}, u32[]{:S(2)}) collective-permute-start(bf16[1,2,96,192]{2,3,1,0:T(8,128)(2,1)S(1)} %fusion.20), channel_id=1, source_target_pairs={{0,2},{1,3},{2,0},{3,1},{4,6},{5,7},{6,4},{7,5},{8,10},{9,11},{10,... | collective-permute-start | bytes 221192 | tf_op jit(solution)/shard_map/ppermute | solution.py:76
  35.7 0.4 fusion.7
  36.1 2.9 %collective-permute-done.10 = bf16[1,2,96,192]{2,3,1,0:T(8,128)(2,1)S(1)} collective-permute-done((bf16[1,2,96,192]{2,3,1,0:T(8,128)(2,1)S(1)}, bf16[1,2,96,192]{2,3,1,0:T(8,128)(2,1)S(1)}, u32[]{:S(2)}, u32[]{:S(2)}) %collective-permute-start.10) | collective-permute-done | bytes 73760 | tf_op jit(solution)/shard_map/ppermute | solution.py:76
  39.0 6.4 %collective-permute-start.11 = (bf16[2,96,192]{1,2,0:T(8,128)(2,1)S(1)}, bf16[2,96,192]{1,2,0:T(8,128)(2,1)S(1)}, u32[]{:S(2)}, u32[]{:S(2)}) collective-permute-start(bf16[2,96,192]{1,2,0:T(8,128)(2,1)S(1)} %fusion.23), channel_id=1, source_target_pairs={{0,0},{1,8},{2,16},{3,24},{4,4},{5,12},{6,20},{7,28},{8,1},{9,9},{... | collective-permute-start | bytes 221192 | tf_op jit(solution)/shard_map/ppermute | solution.py:76
  45.5 4.6 %collective-permute-done.11 = bf16[2,96,192]{1,2,0:T(8,128)(2,1)S(1)} collective-permute-done((bf16[2,96,192]{1,2,0:T(8,128)(2,1)S(1)}, bf16[2,96,192]{1,2,0:T(8,128)(2,1)S(1)}, u32[]{:S(2)}, u32[]{:S(2)}) %collective-permute-start.11) | collective-permute-done | bytes 73760 | tf_op jit(solution)/shard_map/ppermute | solution.py:76
  50.1 0.1 fusion.25
  50.2 0.1 copy.10
  50.3 0.1 copy.9
  50.4 0.8 %pad_maximum_fusion.2 = f32[2,96,192]{2,1,0:T(8,128)} fusion(f32[2,96,96]{2,1,0:T(8,128)S(1)} %bitcast.119, f32[2,96,96]{2,1,0:T(8,128)S(1)} %bitcast.120), kind=kLoop, calls=%fused_computation.47 | loop fusion | flops 36864 | bytes 294912 | tf_op jit(solution)/shard_map/concatenate | solution.py:165
  (12 shorter events, 0.2 us)
Async XLA Ops:
  0.0 22.0 %copy-start.1 = (bf16[2,96,512]{2,1,0:T(8,128)(2,1)S(1)}, bf16[2,96,512]{2,1,0:T(8,128)(2,1)}, u32[]{:S(2)}) copy-start(bf16[2,96,512]{2,1,0:T(8,128)(2,1)} %param.6) | copy-start | bytes 589828
  0.0 9.7 %collective-permute-start = (bf16[2,96,512]{2,1,0:T(8,128)(2,1)}, bf16[2,96,512]{2,1,0:T(8,128)(2,1)S(1)}, u32[]{:S(2)}, u32[]{:S(2)}) collective-permute-start(bf16[2,96,512]{2,1,0:T(8,128)(2,1)} %param.6), channel_id=1, source_target_pairs={{0,4},{1,5},{2,6},{3,7},{4,0},{5,1},{6,2},{7,3},{8,12},{9,13},{10,... | collective-permute-start | bytes 589832 | tf_op jit(solution)/shard_map/ppermute | solution.py:76
  1.5 8.3 %collective-permute-start.2 = (bf16[2,96,512]{2,1,0:T(8,128)(2,1)}, bf16[2,96,512]{2,1,0:T(8,128)(2,1)S(1)}, u32[]{:S(2)}, u32[]{:S(2)}) collective-permute-start(bf16[2,96,512]{2,1,0:T(8,128)(2,1)} %param.6), channel_id=1, source_target_pairs={{0,2},{1,3},{2,0},{3,1},{4,6},{5,7},{6,4},{7,5},{8,10},{9,11},{10,... | collective-permute-start | bytes 589832 | tf_op jit(solution)/shard_map/ppermute | solution.py:76
  2.0 9.8 %collective-permute-start.8 = (bf16[2,96,512]{2,1,0:T(8,128)(2,1)}, bf16[2,96,512]{2,1,0:T(8,128)(2,1)S(1)}, u32[]{:S(2)}, u32[]{:S(2)}) collective-permute-start(bf16[2,96,512]{2,1,0:T(8,128)(2,1)} %param.6), channel_id=1, source_target_pairs={{0,24},{1,25},{2,26},{3,27},{4,28},{5,29},{6,30},{7,31},{8,16},{9,... | collective-permute-start | bytes 589832 | tf_op jit(solution)/shard_map/ppermute | solution.py:76
  5.6 16.3 %collective-permute-start.7 = (bf16[2,96,512]{2,1,0:T(8,128)(2,1)}, bf16[2,96,512]{2,1,0:T(8,128)(2,1)S(1)}, u32[]{:S(2)}, u32[]{:S(2)}) collective-permute-start(bf16[2,96,512]{2,1,0:T(8,128)(2,1)} %param.6), channel_id=1, source_target_pairs={{0,16},{1,17},{2,18},{3,19},{4,20},{5,21},{6,22},{7,23},{8,24},{9,... | collective-permute-start | bytes 589832 | tf_op jit(solution)/shard_map/ppermute | solution.py:76
  5.6 16.3 %collective-permute-start.6 = (bf16[2,96,512]{2,1,0:T(8,128)(2,1)}, bf16[2,96,512]{2,1,0:T(8,128)(2,1)S(1)}, u32[]{:S(2)}, u32[]{:S(2)}) collective-permute-start(bf16[2,96,512]{2,1,0:T(8,128)(2,1)} %param.6), channel_id=1, source_target_pairs={{0,8},{1,9},{2,10},{3,11},{4,12},{5,13},{6,14},{7,15},{8,0},{9,1},... | collective-permute-start | bytes 589832 | tf_op jit(solution)/shard_map/ppermute | solution.py:76
  8.4 15.5 %copy-start = (bf16[2,2,512,2048]{3,2,1,0:T(8,128)(2,1)S(1)}, bf16[2,2,512,2048]{3,2,1,0:T(8,128)(2,1)}, u32[]{:S(2)}) copy-start(bf16[2,2,512,2048]{3,2,1,0:T(8,128)(2,1)} %refs_4_.1) | copy-start | bytes 25165828
  9.8 12.7 %collective-permute-start.1 = (bf16[2,192,512]{2,1,0:T(8,128)(2,1)S(1)}, bf16[2,192,512]{2,1,0:T(8,128)(2,1)S(1)}, u32[]{:S(2)}, u32[]{:S(2)}) collective-permute-start(bf16[2,192,512]{2,1,0:T(8,128)(2,1)S(1)} %constant_dynamic-update-slice_fusion.refs_0_), channel_id=1, source_target_pairs={{0,1},{1,0},{2,3},{3,2},{4,5},{5,4},{6,7},{7,6},{8,9},{9,8},{10,11... | collective-permute-start | bytes 1179656 | tf_op jit(solution)/shard_map/ppermute | solution.py:76
  9.9 12.2 %collective-permute-start.4 = (bf16[96,512]{1,0:T(8,128)(2,1)S(1)}, bf16[96,512]{1,0:T(8,128)(2,1)S(1)}, u32[]{:S(2)}, u32[]{:S(2)}) collective-permute-start(bf16[96,512]{1,0:T(8,128)(2,1)S(1)} %slice_bitcast_fusion.3), channel_id=1, source_target_pairs={{0,4},{1,5},{2,6},{3,7},{4,0},{5,1},{6,2},{7,3},{8,12},{9,13},{10,... | collective-permute-start | bytes 294920 | tf_op jit(solution)/shard_map/ppermute | solution.py:76
  11.8 10.2 %collective-permute-start.3 = (bf16[96,512]{1,0:T(8,128)(2,1)S(1)}, bf16[96,512]{1,0:T(8,128)(2,1)S(1)}, u32[]{:S(2)}, u32[]{:S(2)}) collective-permute-start(bf16[96,512]{1,0:T(8,128)(2,1)S(1)} %slice_bitcast_fusion.4), channel_id=1, source_target_pairs={{0,2},{1,3},{2,0},{3,1},{4,6},{5,7},{6,4},{7,5},{8,10},{9,11},{10,... | collective-permute-start | bytes 294920 | tf_op jit(solution)/shard_map/ppermute | solution.py:76
  22.1 1.8 %collective-permute-start.5 = (bf16[2,192,512]{2,1,0:T(8,128)(2,1)S(1)}, bf16[2,192,512]{2,1,0:T(8,128)(2,1)S(1)}, u32[]{:S(2)}, u32[]{:S(2)}) collective-permute-start(bf16[2,192,512]{2,1,0:T(8,128)(2,1)S(1)} %maximum_maximum_fusion.refs_2_), channel_id=1, source_target_pairs={{0,1},{1,0},{2,3},{3,2},{4,5},{5,4},{6,7},{7,6},{8,9},{9,8},{10,11... | collective-permute-start | bytes 1179656 | tf_op jit(solution)/shard_map/ppermute | solution.py:76
  32.3 1.8 %collective-permute-start.9 = (f32[2,2,96,192]{2,3,1,0:T(8,128)S(1)}, f32[2,2,96,192]{2,3,1,0:T(8,128)S(1)}, u32[]{:S(2)}, u32[]{:S(2)}) collective-permute-start(f32[2,2,96,192]{2,3,1,0:T(8,128)S(1)} %pad_maximum_fusion.1), channel_id=1, source_target_pairs={{0,1},{1,0},{2,3},{3,2},{4,5},{5,4},{6,7},{7,6},{8,9},{9,8},{10,11... | collective-permute-start | bytes 884744 | tf_op jit(solution)/shard_map/ppermute | solution.py:76
  34.1 4.9 %collective-permute-start.10 = (bf16[1,2,96,192]{2,3,1,0:T(8,128)(2,1)S(1)}, bf16[1,2,96,192]{2,3,1,0:T(8,128)(2,1)S(1)}, u32[]{:S(2)}, u32[]{:S(2)}) collective-permute-start(bf16[1,2,96,192]{2,3,1,0:T(8,128)(2,1)S(1)} %fusion.20), channel_id=1, source_target_pairs={{0,2},{1,3},{2,0},{3,1},{4,6},{5,7},{6,4},{7,5},{8,10},{9,11},{10,... | collective-permute-start | bytes 221192 | tf_op jit(solution)/shard_map/ppermute | solution.py:76
  39.0 11.0 %collective-permute-start.11 = (bf16[2,96,192]{1,2,0:T(8,128)(2,1)S(1)}, bf16[2,96,192]{1,2,0:T(8,128)(2,1)S(1)}, u32[]{:S(2)}, u32[]{:S(2)}) collective-permute-start(bf16[2,96,192]{1,2,0:T(8,128)(2,1)S(1)} %fusion.23), channel_id=1, source_target_pairs={{0,0},{1,8},{2,16},{3,24},{4,4},{5,12},{6,20},{7,28},{8,1},{9,9},{... | collective-permute-start | bytes 221192 | tf_op jit(solution)/shard_map/ppermute | solution.py:76

commit v2 on v1

--- a/solution.py
+++ b/solution.py
@@ -14,42 +14,49 @@
     _, m, k = pieces[0].shape
     freqs, _, g, total = screened.shape
     tile = min(g, 256)
+    steps = [(w, t) for w in range(freqs) for t in range(0, g, tile)]
 
     def kernel(order_ref, *refs):
-        piece_refs, w_ref, out_ref = refs[:count], refs[count], refs[count + 1]
-        real, imag, minus = refs[count + 2:]
-
-        @pl.when((pl.program_id(0) == 0) & (pl.program_id(1) == 0))
-        def _():
-            for j in range(count):
-                columns = pl.ds(pl.multiple_of(order_ref[j] * k, k), k)
-                real[:, columns] = piece_refs[j][0]
-                imag[:, columns] = piece_refs[j][1]
-                minus[:, columns] = -piece_refs[j][1]
+        piece_refs, w_hbm, out_ref = refs[:count], refs[count], refs[count + 1]
+        w_ref, real, imag, minus, sems = refs[count + 2:]
+        copies = [
+            pltpu.make_async_copy(
+                w_hbm.at[w, :, pl.ds(t, tile), :], w_ref.at[i], sems.at[i]
+            )
+            for i, (w, t) in enumerate(steps)
+        ]
+        for copy in copies:
+            copy.start()
+        for j in range(count):
+            columns = pl.ds(pl.multiple_of(order_ref[j] * k, k), k)
+            real[:, columns] = piece_refs[j][0]
+            imag[:, columns] = piece_refs[j][1]
+            minus[:, columns] = -piece_refs[j][1]
 
         def dot(left, right):
             return lax.dot_general(
                 left, right, (((1,), (1,)), ((), ())), preferred_element_type=jnp.float32
             )
 
-        first = dot(real[...], w_ref[0, 0]) + dot(minus[...], w_ref[0, 1])
-        out_ref[0, 0] = first.astype(jnp.bfloat16)
-        second = dot(imag[...], w_ref[0, 0]) + dot(real[...], w_ref[0, 1])
-        out_ref[0, 1] = second.astype(jnp.bfloat16)
+        for i, (w, t) in enumerate(steps):
+            copies[i].wait()
+            first = dot(real[...], w_ref[i, 0]) + dot(minus[...], w_ref[i, 1])
+            out_ref[w, 0, :, pl.ds(t, tile)] = first.astype(jnp.bfloat16)
+            second = dot(imag[...], w_ref[i, 0]) + dot(real[...], w_ref[i, 1])
+            out_ref[w, 1, :, pl.ds(t, tile)] = second.astype(jnp.bfloat16)
 
-    whole = pl.BlockSpec((2, m, k), lambda w, t, order_ref: (0, 0, 0))
+    in_vmem = pl.BlockSpec(memory_space=pltpu.VMEM)
     return pl.pallas_call(
         kernel,
-        grid_spec=pltpu.PrefetchScalarGridSpec(
-            num_scalar_prefetch=1,
-            grid=(freqs, g // tile),
-            in_specs=[whole] * count
-            + [pl.BlockSpec((1, 2, tile, total), lambda w, t, order_ref: (w, 0, t, 0))],
-            out_specs=pl.BlockSpec((1, 2, m, tile), lambda w, t, order_ref: (w, 0, 0, t)),
-            scratch_shapes=[pltpu.VMEM((m, total), jnp.bfloat16)] * 3,
-        ),
+        in_specs=[pl.BlockSpec(memory_space=pltpu.SMEM)]
+        + [in_vmem] * count
+        + [pl.BlockSpec(memory_space=pltpu.HBM)],
+        out_specs=in_vmem,
+        scratch_shapes=[pltpu.VMEM((len(steps), 2, tile, total), jnp.bfloat16)]
+        + [pltpu.VMEM((m, total), jnp.bfloat16)] * 3
+        + [pltpu.SemaphoreType.DMA((len(steps),))],
         out_shape=jax.ShapeDtypeStruct((freqs, 2, m, g), jnp.bfloat16),
-        compiler_params=pltpu.CompilerParams(vmem_limit_bytes=40 * 2**20),
+        compiler_params=pltpu.CompilerParams(vmem_limit_bytes=57 * 2**20),
         cost_estimate=pl.CostEstimate(
             flops=8 * freqs * m * g * total,
             bytes_accessed=2 * screened.size + 4 * freqs * m * g + 4 * m * total,
@@ -99,10 +106,10 @@
         at = [elements]
         for o in range(1, A):
             at.append(move(elements, swap(o)))
-        both = [
-            jnp.stack([move(piece[0], flip(high)), move(across[1], turn(o))])
-            for o, piece in zip(range(1, R), beside)
-        ]
+        both = []
+        for o, piece in zip(range(1, R), beside):
+            one = move(piece[0], flip(high))
+            both.append(jnp.stack([one, move(across[1], turn(o))]))
         mine = jnp.concatenate([elements] + beside, axis=1)
         far = jnp.concatenate([across] + both, axis=1)
         known = {0: mine, high: far}
@@ -128,6 +135,7 @@
         at = jnp.stack(at)
         turned = [lax.dynamic_index_in_dim(at, row ^ a ^ j, 0, keepdims=False) for j in range(A)]
 
+        band_of_slot, energies, _ = lax.optimization_barrier((band_of_slot, energies, far))
         if small(R):
             hit = band_of_slot[None, :] == lax.iota(jnp.int32, energies.shape[0])[:, None]
             slot_energy = jnp.sum(jnp.where(hit, energies[:, None], 0.0), axis=0)

time: 51.4 us -> 57.5 us (1.12)
  Pallas kernels: 7.54 us -> 10 us
  matrix products: 1.57 us -> 3.93 us
  local copies, waits for them, and re-layouts: 1.48 us -> 2.53 us
  starting transfers between devices: 16.6 us -> 15.7 us
  waiting for transfers between devices: 20.3 us -> 21.2 us
    pallas_call x1, Pallas kernels: 7.54 us -> 10 us  [apply_screened(): pl.pallas_call(kernel, in_specs=[pl.BlockSpec(memory_space=pltpu.SMEM)] +...]
    dot_general x4, matrix products: 1.57 us -> 3.93 us  [on_device(): jnp.einsum('dcnk,wcmk->wdnm', left, applied, preferred_element_type=jnp.f...]
    unnamed x5 -> x19, local copies, waits for them, and re-layouts: 1.1 us -> 2.15 us
    another operation x1, other arithmetic: 0.1 us -> 1.03 us  [on_device(): at = jnp.stack(at)]
    ppermute x12, waiting for transfers between devices: 20.3 us -> 21.2 us  [move(): return lax.ppermute(value, BOTH, pairs)]
    ppermute x12, starting transfers between devices: 16.6 us -> 15.7 us  [move(): return lax.ppermute(value, BOTH, pairs)]
    reduce_sum x1, other arithmetic: 1.05 us -> 0.35 us  [on_device(): slot_energy = jnp.sum(jnp.where(hit, energies[:, None], 0.0), axis=0)]
    div x1, other arithmetic: 0.75 us -> 0.08 us  [on_device(): screen = freq_weights[:, None] / (1.0 + 4.0 * offset * offset)]
  transfers between devices with their start and end apart: 12 -> 12, of which waited for: 6 -> 6; matrix products, arithmetic and copies ran while one was open for 9% -> 8% of each run, Pallas kernels for 0% -> 0%
where the time goes in v2:
time: 57.5 us; the launch traced here: 57.2 us
  waiting for transfers between devices  21.2 us (37%)
  starting transfers between devices  15.7 us (27%)
  Pallas kernels  10 us (17%)
  matrix products  3.93 us (7%)
  other arithmetic  3.37 us (6%)
  local copies, waits for them, and re-layouts  2.53 us (4%)
    ppermute x12, waiting for transfers between devices, move(): return lax.ppermute(value, BOTH, pairs)  21.2 us
    ppermute x12, starting transfers between devices, move(): return lax.ppermute(value, BOTH, pairs)  15.7 us
    pallas_call x1, Pallas kernels, apply_screened(): pl.pallas_call(kernel, in_specs=[pl.BlockSpec(memory_space=pltpu.SMEM)] +...  10 us
    dot_general x4, matrix products, on_device(): jnp.einsum('dcnk,wcmk->wdnm', left, applied, preferred_element_type=jnp.f...  3.93 us
    unnamed x19, local copies, waits for them, and re-layouts  2.15 us
  transfers between devices with their start and end apart: 12, of which 6 were waited for; matrix products, arithmetic and copies ran while one was open for 8% of the time, Pallas kernels for 0%

profile of v2, /device:TPU:4, one launch (start us, length us, event | category | flops | bytes accessed | tf_op | source)
XLA Modules:
  0.0 57.2 jit_solution(6623390079216877258)
XLA Ops:
  0.0 1.5 %collective-permute-start = (bf16[2,96,512]{2,1,0:T(8,128)(2,1)}, bf16[2,96,512]{2,1,0:T(8,128)(2,1)S(1)}, u32[]{:S(2)}, u32[]{:S(2)}) collective-permute-start(bf16[2,96,512]{2,1,0:T(8,128)(2,1)} %param.6), channel_id=1, source_target_pairs={{0,4},{1,5},{2,6},{3,7},{4,0},{5,1},{6,2},{7,3},{8,12},{9,13},{10,... | collective-permute-start | bytes 589832 | tf_op jit(solution)/shard_map/ppermute | solution.py:83
  1.5 0.5 collective-permute-start.2
  2.0 3.6 %collective-permute-start.8 = (bf16[2,96,512]{2,1,0:T(8,128)(2,1)}, bf16[2,96,512]{2,1,0:T(8,128)(2,1)S(1)}, u32[]{:S(2)}, u32[]{:S(2)}) collective-permute-start(bf16[2,96,512]{2,1,0:T(8,128)(2,1)} %param.6), channel_id=1, source_target_pairs={{0,24},{1,25},{2,26},{3,27},{4,28},{5,29},{6,30},{7,31},{8,16},{9,... | collective-permute-start | bytes 589832 | tf_op jit(solution)/shard_map/ppermute | solution.py:83
  5.6 0.0 collective-permute-start.7
  5.6 0.8 %collective-permute-start.6 = (bf16[2,96,512]{2,1,0:T(8,128)(2,1)}, bf16[2,96,512]{2,1,0:T(8,128)(2,1)S(1)}, u32[]{:S(2)}, u32[]{:S(2)}) collective-permute-start(bf16[2,96,512]{2,1,0:T(8,128)(2,1)} %param.6), channel_id=1, source_target_pairs={{0,8},{1,9},{2,10},{3,11},{4,12},{5,13},{6,14},{7,15},{8,0},{9,1},... | collective-permute-start | bytes 589832 | tf_op jit(solution)/shard_map/ppermute | solution.py:83
  6.4 1.0 %constant_dynamic-update-slice_fusion.1 = bf16[2,192,512]{2,1,0:T(8,128)(2,1)S(1)} fusion(bf16[2,96,512]{2,1,0:T(8,128)(2,1)} %param.6), kind=kLoop, calls=%fused_computation.74 | loop fusion | bytes 393216
  7.4 0.6 %pad_add_fusion.order_ref = s32[4]{0:T(128)} fusion(s32[1]{0:T(128)} %bitcast.3, s32[1]{0:T(128)} %bitcast.2, s32[1]{0:T(128)} %bitcast.1, s32[1]{0:T(128)} %bitcast), kind=kLoop, calls=%fused_computation.86 | loop fusion | flops 12 | bytes 32 | tf_op jit(solution)/shard_map/stack | solution.py:122
  8.0 0.1 collective-permute-start.1
  8.1 0.0 collective-permute-done.2
  8.1 0.6 %collective-permute-start.4 = (bf16[96,512]{1,0:T(8,128)(2,1)S(1)}, bf16[96,512]{1,0:T(8,128)(2,1)S(1)}, u32[]{:S(2)}, u32[]{:S(2)}) collective-permute-start(bf16[96,512]{1,0:T(8,128)(2,1)S(1)} %slice_bitcast_fusion.3), channel_id=1, source_target_pairs={{0,4},{1,5},{2,6},{3,7},{4,0},{5,1},{6,2},{7,3},{8,12},{9,13},{10,... | collective-permute-start | bytes 294920 | tf_op jit(solution)/shard_map/ppermute | solution.py:83
  8.7 3.2 %collective-permute-done.8 = bf16[2,96,512]{2,1,0:T(8,128)(2,1)S(1)} collective-permute-done((bf16[2,96,512]{2,1,0:T(8,128)(2,1)}, bf16[2,96,512]{2,1,0:T(8,128)(2,1)S(1)}, u32[]{:S(2)}, u32[]{:S(2)}) %collective-permute-start.8) | collective-permute-done | bytes 196640 | tf_op jit(solution)/shard_map/ppermute | solution.py:83
  11.8 1.5 %collective-permute-start.3 = (bf16[96,512]{1,0:T(8,128)(2,1)S(1)}, bf16[96,512]{1,0:T(8,128)(2,1)S(1)}, u32[]{:S(2)}, u32[]{:S(2)}) collective-permute-start(bf16[96,512]{1,0:T(8,128)(2,1)S(1)} %slice_bitcast_fusion.4), channel_id=1, source_target_pairs={{0,2},{1,3},{2,0},{3,1},{4,6},{5,7},{6,4},{7,5},{8,10},{9,11},{10,... | collective-permute-start | bytes 294920 | tf_op jit(solution)/shard_map/ppermute | solution.py:83
  13.4 8.6 %collective-permute-done.7 = bf16[2,96,512]{2,1,0:T(8,128)(2,1)S(1)} collective-permute-done((bf16[2,96,512]{2,1,0:T(8,128)(2,1)}, bf16[2,96,512]{2,1,0:T(8,128)(2,1)S(1)}, u32[]{:S(2)}, u32[]{:S(2)}) %collective-permute-start.7) | collective-permute-done | bytes 196640 | tf_op jit(solution)/shard_map/ppermute | solution.py:83
  21.9 1.0 %pad_maximum_fusion = bf16[4,2,96,512]{3,2,1,0:T(8,128)(2,1)S(1)} fusion(bf16[1,2,96,512]{3,2,1,0:T(8,128)(2,1)S(1)} %bitcast.121, bf16[1,2,96,512]{3,2,1,0:T(8,128)(2,1)S(1)} %bitcast.122, bf16[1,2,96,512]{3,2,1,0:T(8,128)(2,1)S(1)} %bitcast.123, bf16[1,2,96,512]{3,2,1,0:T(8,128)(2,1)} %bitcast.118), kind=kLoop, calls=%fused_computation.14 | loop fusion | flops 1179648 | bytes 1572864 | tf_op jit(solution)/shard_map/stack | solution.py:135
  23.0 0.0 copy-start.2
  23.0 0.0 copy-start.3
  23.0 0.0 copy-start.4
  23.0 0.0 copy-start.5
  23.0 0.1 constant_dynamic-slice_fusion.1
  23.1 0.1 fusion.26
  23.3 0.0 collective-permute-done.4
  23.3 0.0 collective-permute-done.3
  23.3 0.1 collective-permute-start.5
  23.4 0.3 copy-done.2
  23.7 0.0 copy-done.3
  23.7 0.3 select_reduce_fusion
  24.1 0.1 fusion.31
  24.1 0.1 constant_dynamic-slice_fusion
  24.2 0.1 pad_maximum_fusion.3
  24.3 0.1 add_multiply_fusion
  24.5 0.6 %collective-permute-done.5.refs_3_ = bf16[2,192,512]{2,1,0:T(8,128)(2,1)S(1)} collective-permute-done((bf16[2,192,512]{2,1,0:T(8,128)(2,1)S(1)}, bf16[2,192,512]{2,1,0:T(8,128)(2,1)S(1)}, u32[]{:S(2)}, u32[]{:S(2)}) %collective-permute-start.5) | collective-permute-done | bytes 393248 | tf_op jit(solution)/shard_map/ppermute | solution.py:83
  25.1 0.1 copy-done.6
  25.2 0.7 %copy-done.7 = bf16[2,192,512]{2,1,0:T(8,128)(2,1)} copy-done((bf16[2,192,512]{2,1,0:T(8,128)(2,1)}, bf16[2,192,512]{2,1,0:T(8,128)(2,1)S(1)}, u32[]{:S(2)}) %copy-start.7) | copy-done | bytes 393240
  26.0 10.0 %shard_map.64 = bf16[2,2,192,512]{3,2,1,0:T(8,128)(2,1)} custom-call(s32[4]{0:T(128)} %pad_add_fusion.order_ref, bf16[2,192,512]{2,1,0:T(8,128)(2,1)} %copy-done.1, bf16[2,192,512]{2,1,0:T(8,128)(2,1)} %copy-done.6, bf16[2,192,512]{2,1,0:T(8,128)(2,1)} %copy-done, bf16[2,192,512]{2,1,0:T(8,128)(2,1)} %copy-done.7, bf16[2,2,512,2048]{3,2,1,0:T(8,128)(2,1)} %refs_4_.1), custom_call_target="tpu_custom_call" | custom-call | flops 3221225472 | bytes 10747904 | tf_op jit(solution)/shard_map/pallas_call | solution.py:49
  36.0 1.6 %fusion.5 = f32[2,96,192]{1,2,0:T(8,128)S(1)} fusion(bf16[2,2,192,512]{3,2,1,0:T(8,128)(2,1)} %shard_map.64, bf16[1,2,96,512]{3,2,1,0:T(8,128)(2,1)S(1)} %get-tuple-element.36, bf16[1,2,96,512]{3,2,1,0:T(8,128)(2,1)S(1)} %get-tuple-element.10, f32[2,96,192]{1,2,0:T(8,128)S(1)} %get-tuple-element.33), kind=kOutput, calls=%fused_computation.11 | convolution fusion | flops 151891968 | bytes 1474560 | tf_op jit(solution)/shard_map/dcnk,wcmk->wdnm/dot_general | solution.py:155
  37.6 1.5 %fusion.6 = f32[2,96,192]{1,2,0:T(8,128)S(1)} fusion(bf16[2,2,192,512]{3,2,1,0:T(8,128)(2,1)} %shard_map.64, bf16[1,2,96,512]{3,2,1,0:T(8,128)(2,1)S(1)} %get-tuple-element.35, bf16[1,2,96,512]{3,2,1,0:T(8,128)(2,1)S(1)} %get-tuple-element.11, f32[2,96,192]{1,2,0:T(8,128)S(1)} %get-tuple-element.32), kind=kOutput, calls=%fused_computation.12 | convolution fusion | flops 151891968 | bytes 1474560 | tf_op jit(solution)/shard_map/dcnk,wcmk->wdnm/dot_general | solution.py:155
  39.2 0.3 collective-permute-start.9
  39.5 0.4 fusion.4
  39.9 1.1 %collective-permute-done.9 = f32[2,2,96,192]{2,3,1,0:T(8,128)S(1)} collective-permute-done((f32[2,2,96,192]{2,3,1,0:T(8,128)S(1)}, f32[2,2,96,192]{2,3,1,0:T(8,128)S(1)}, u32[]{:S(2)}, u32[]{:S(2)}) %collective-permute-start.9) | collective-permute-done | bytes 294944 | tf_op jit(solution)/shard_map/ppermute | solution.py:83
  41.0 1.6 %collective-permute-start.10 = (bf16[1,2,96,192]{2,3,1,0:T(8,128)(2,1)S(1)}, bf16[1,2,96,192]{2,3,1,0:T(8,128)(2,1)S(1)}, u32[]{:S(2)}, u32[]{:S(2)}) collective-permute-start(bf16[1,2,96,192]{2,3,1,0:T(8,128)(2,1)S(1)} %fusion.20), channel_id=1, source_target_pairs={{0,2},{1,3},{2,0},{3,1},{4,6},{5,7},{6,4},{7,5},{8,10},{9,11},{10,... | collective-permute-start | bytes 221192 | tf_op jit(solution)/shard_map/ppermute | solution.py:83
  42.6 0.4 fusion.7
  43.0 3.0 %collective-permute-done.10 = bf16[1,2,96,192]{2,3,1,0:T(8,128)(2,1)S(1)} collective-permute-done((bf16[1,2,96,192]{2,3,1,0:T(8,128)(2,1)S(1)}, bf16[1,2,96,192]{2,3,1,0:T(8,128)(2,1)S(1)}, u32[]{:S(2)}, u32[]{:S(2)}) %collective-permute-start.10) | collective-permute-done | bytes 73760 | tf_op jit(solution)/shard_map/ppermute | solution.py:83
  46.0 5.2 %collective-permute-start.11 = (bf16[2,96,192]{1,2,0:T(8,128)(2,1)S(1)}, bf16[2,96,192]{1,2,0:T(8,128)(2,1)S(1)}, u32[]{:S(2)}, u32[]{:S(2)}) collective-permute-start(bf16[2,96,192]{1,2,0:T(8,128)(2,1)S(1)} %fusion.23), channel_id=1, source_target_pairs={{0,0},{1,8},{2,16},{3,24},{4,4},{5,12},{6,20},{7,28},{8,1},{9,9},{... | collective-permute-start | bytes 221192 | tf_op jit(solution)/shard_map/ppermute | solution.py:83
  51.3 4.8 %collective-permute-done.11 = bf16[2,96,192]{1,2,0:T(8,128)(2,1)S(1)} collective-permute-done((bf16[2,96,192]{1,2,0:T(8,128)(2,1)S(1)}, bf16[2,96,192]{1,2,0:T(8,128)(2,1)S(1)}, u32[]{:S(2)}, u32[]{:S(2)}) %collective-permute-start.11) | collective-permute-done | bytes 73760 | tf_op jit(solution)/shard_map/ppermute | solution.py:83
  56.1 0.1 fusion.25
  56.2 0.1 copy.10
  56.3 0.1 copy.9
  56.4 0.8 %pad_maximum_fusion.2 = f32[2,96,192]{2,1,0:T(8,128)} fusion(f32[2,96,96]{2,1,0:T(8,128)S(1)} %bitcast.119, f32[2,96,96]{2,1,0:T(8,128)S(1)} %bitcast.120), kind=kLoop, calls=%fused_computation.47 | loop fusion | flops 36864 | bytes 294912 | tf_op jit(solution)/shard_map/concatenate | solution.py:173
  (25 shorter events, 0.3 us)
Async XLA Ops:
  0.0 8.0 %collective-permute-start = (bf16[2,96,512]{2,1,0:T(8,128)(2,1)}, bf16[2,96,512]{2,1,0:T(8,128)(2,1)S(1)}, u32[]{:S(2)}, u32[]{:S(2)}) collective-permute-start(bf16[2,96,512]{2,1,0:T(8,128)(2,1)} %param.6), channel_id=1, source_target_pairs={{0,4},{1,5},{2,6},{3,7},{4,0},{5,1},{6,2},{7,3},{8,12},{9,13},{10,... | collective-permute-start | bytes 589832 | tf_op jit(solution)/shard_map/ppermute | solution.py:83
  1.5 6.6 %collective-permute-start.2 = (bf16[2,96,512]{2,1,0:T(8,128)(2,1)}, bf16[2,96,512]{2,1,0:T(8,128)(2,1)S(1)}, u32[]{:S(2)}, u32[]{:S(2)}) collective-permute-start(bf16[2,96,512]{2,1,0:T(8,128)(2,1)} %param.6), channel_id=1, source_target_pairs={{0,2},{1,3},{2,0},{3,1},{4,6},{5,7},{6,4},{7,5},{8,10},{9,11},{10,... | collective-permute-start | bytes 589832 | tf_op jit(solution)/shard_map/ppermute | solution.py:83
  2.0 9.8 %collective-permute-start.8 = (bf16[2,96,512]{2,1,0:T(8,128)(2,1)}, bf16[2,96,512]{2,1,0:T(8,128)(2,1)S(1)}, u32[]{:S(2)}, u32[]{:S(2)}) collective-permute-start(bf16[2,96,512]{2,1,0:T(8,128)(2,1)} %param.6), channel_id=1, source_target_pairs={{0,24},{1,25},{2,26},{3,27},{4,28},{5,29},{6,30},{7,31},{8,16},{9,... | collective-permute-start | bytes 589832 | tf_op jit(solution)/shard_map/ppermute | solution.py:83
  5.6 16.3 %collective-permute-start.7 = (bf16[2,96,512]{2,1,0:T(8,128)(2,1)}, bf16[2,96,512]{2,1,0:T(8,128)(2,1)S(1)}, u32[]{:S(2)}, u32[]{:S(2)}) collective-permute-start(bf16[2,96,512]{2,1,0:T(8,128)(2,1)} %param.6), channel_id=1, source_target_pairs={{0,16},{1,17},{2,18},{3,19},{4,20},{5,21},{6,22},{7,23},{8,24},{9,... | collective-permute-start | bytes 589832 | tf_op jit(solution)/shard_map/ppermute | solution.py:83
  5.6 16.3 %collective-permute-start.6 = (bf16[2,96,512]{2,1,0:T(8,128)(2,1)}, bf16[2,96,512]{2,1,0:T(8,128)(2,1)S(1)}, u32[]{:S(2)}, u32[]{:S(2)}) collective-permute-start(bf16[2,96,512]{2,1,0:T(8,128)(2,1)} %param.6), channel_id=1, source_target_pairs={{0,8},{1,9},{2,10},{3,11},{4,12},{5,13},{6,14},{7,15},{8,0},{9,1},... | collective-permute-start | bytes 589832 | tf_op jit(solution)/shard_map/ppermute | solution.py:83
  8.0 15.2 %copy-start.1 = (bf16[2,192,512]{2,1,0:T(8,128)(2,1)}, bf16[2,192,512]{2,1,0:T(8,128)(2,1)S(1)}, u32[]{:S(2)}) copy-start(bf16[2,192,512]{2,1,0:T(8,128)(2,1)S(1)} %constant_dynamic-update-slice_fusion.refs_0_) | copy-start | bytes 1179652
  8.0 16.5 %collective-permute-start.1 = (bf16[2,192,512]{2,1,0:T(8,128)(2,1)S(1)}, bf16[2,192,512]{2,1,0:T(8,128)(2,1)S(1)}, u32[]{:S(2)}, u32[]{:S(2)}) collective-permute-start(bf16[2,192,512]{2,1,0:T(8,128)(2,1)S(1)} %constant_dynamic-update-slice_fusion.refs_0_), channel_id=1, source_target_pairs={{0,1},{1,0},{2,3},{3,2},{4,5},{5,4},{6,7},{7,6},{8,9},{9,8},{10,11... | collective-permute-start | bytes 1179656 | tf_op jit(solution)/shard_map/ppermute | solution.py:83
  8.1 15.2 %collective-permute-start.4 = (bf16[96,512]{1,0:T(8,128)(2,1)S(1)}, bf16[96,512]{1,0:T(8,128)(2,1)S(1)}, u32[]{:S(2)}, u32[]{:S(2)}) collective-permute-start(bf16[96,512]{1,0:T(8,128)(2,1)S(1)} %slice_bitcast_fusion.3), channel_id=1, source_target_pairs={{0,4},{1,5},{2,6},{3,7},{4,0},{5,1},{6,2},{7,3},{8,12},{9,13},{10,... | collective-permute-start | bytes 294920 | tf_op jit(solution)/shard_map/ppermute | solution.py:83
  11.8 11.4 %collective-permute-start.3 = (bf16[96,512]{1,0:T(8,128)(2,1)S(1)}, bf16[96,512]{1,0:T(8,128)(2,1)S(1)}, u32[]{:S(2)}, u32[]{:S(2)}) collective-permute-start(bf16[96,512]{1,0:T(8,128)(2,1)S(1)} %slice_bitcast_fusion.4), channel_id=1, source_target_pairs={{0,2},{1,3},{2,0},{3,1},{4,6},{5,7},{6,4},{7,5},{8,10},{9,11},{10,... | collective-permute-start | bytes 294920 | tf_op jit(solution)/shard_map/ppermute | solution.py:83
  23.0 0.7 %copy-start.2 = (f32[768]{0:T(1024)S(1)}, f32[768]{0:T(1024)}, u32[]{:S(2)}) copy-start(f32[768]{0:T(1024)} %param.8) | copy-start | bytes 9220
  23.0 0.7 %copy-start.3 = (s32[768]{0:T(1024)S(1)}, s32[768]{0:T(1024)}, u32[]{:S(2)}) copy-start(s32[768]{0:T(1024)} %param.11) | copy-start | bytes 9220
  23.0 1.0 %copy-start.4 = (f32[2]{0:T(128)S(1)}, f32[2]{0:T(128)}, u32[]{:S(2)}) copy-start(f32[2]{0:T(128)} %param.10) | copy-start | bytes 28
  23.0 1.0 %copy-start.5 = (f32[2]{0:T(128)S(1)}, f32[2]{0:T(128)}, u32[]{:S(2)}) copy-start(f32[2]{0:T(128)} %param.9) | copy-start | bytes 28
  23.3 1.8 %copy-start = (bf16[2,192,512]{2,1,0:T(8,128)(2,1)}, bf16[2,192,512]{2,1,0:T(8,128)(2,1)S(1)}, u32[]{:S(2)}) copy-start(bf16[2,192,512]{2,1,0:T(8,128)(2,1)S(1)} %maximum_maximum_fusion.refs_2_) | copy-start | bytes 1179652
  23.3 1.8 %collective-permute-start.5 = (bf16[2,192,512]{2,1,0:T(8,128)(2,1)S(1)}, bf16[2,192,512]{2,1,0:T(8,128)(2,1)S(1)}, u32[]{:S(2)}, u32[]{:S(2)}) collective-permute-start(bf16[2,192,512]{2,1,0:T(8,128)(2,1)S(1)} %maximum_maximum_fusion.refs_2_), channel_id=1, source_target_pairs={{0,1},{1,0},{2,3},{3,2},{4,5},{5,4},{6,7},{7,6},{8,9},{9,8},{10,11... | collective-permute-start | bytes 1179656 | tf_op jit(solution)/shard_map/ppermute | solution.py:83
  24.5 0.8 %copy-start.6 = (bf16[2,192,512]{2,1,0:T(8,128)(2,1)}, bf16[2,192,512]{2,1,0:T(8,128)(2,1)S(1)}, u32[]{:S(2)}) copy-start(bf16[2,192,512]{2,1,0:T(8,128)(2,1)S(1)} %collective-permute-done.1.refs_1_) | copy-start | bytes 1179652
  25.2 0.7 %copy-start.7 = (bf16[2,192,512]{2,1,0:T(8,128)(2,1)}, bf16[2,192,512]{2,1,0:T(8,128)(2,1)S(1)}, u32[]{:S(2)}) copy-start(bf16[2,192,512]{2,1,0:T(8,128)(2,1)S(1)} %collective-permute-done.5.refs_3_) | copy-start | bytes 1179652
  36.0 3.5 %copy-start.8 = (bf16[2,2,192,512]{3,2,1,0:T(8,128)(2,1)S(1)}, bf16[2,2,192,512]{3,2,1,0:T(8,128)(2,1)}, u32[]{:S(2)}) copy-start(bf16[2,2,192,512]{3,2,1,0:T(8,128)(2,1)} %shard_map.64) | copy-start | bytes 2359300
  39.2 1.8 %collective-permute-start.9 = (f32[2,2,96,192]{2,3,1,0:T(8,128)S(1)}, f32[2,2,96,192]{2,3,1,0:T(8,128)S(1)}, u32[]{:S(2)}, u32[]{:S(2)}) collective-permute-start(f32[2,2,96,192]{2,3,1,0:T(8,128)S(1)} %pad_maximum_fusion.1), channel_id=1, source_target_pairs={{0,1},{1,0},{2,3},{3,2},{4,5},{5,4},{6,7},{7,6},{8,9},{9,8},{10,11... | collective-permute-start | bytes 884744 | tf_op jit(solution)/shard_map/ppermute | solution.py:83
  41.0 5.0 %collective-permute-start.10 = (bf16[1,2,96,192]{2,3,1,0:T(8,128)(2,1)S(1)}, bf16[1,2,96,192]{2,3,1,0:T(8,128)(2,1)S(1)}, u32[]{:S(2)}, u32[]{:S(2)}) collective-permute-start(bf16[1,2,96,192]{2,3,1,0:T(8,128)(2,1)S(1)} %fusion.20), channel_id=1, source_target_pairs={{0,2},{1,3},{2,0},{3,1},{4,6},{5,7},{6,4},{7,5},{8,10},{9,11},{10,... | collective-permute-start | bytes 221192 | tf_op jit(solution)/shard_map/ppermute | solution.py:83
  46.0 10.0 %collective-permute-start.11 = (bf16[2,96,192]{1,2,0:T(8,128)(2,1)S(1)}, bf16[2,96,192]{1,2,0:T(8,128)(2,1)S(1)}, u32[]{:S(2)}, u32[]{:S(2)}) collective-permute-start(bf16[2,96,192]{1,2,0:T(8,128)(2,1)S(1)} %fusion.23), channel_id=1, source_target_pairs={{0,0},{1,8},{2,16},{3,24},{4,4},{5,12},{6,20},{7,28},{8,1},{9,9},{... | collective-permute-start | bytes 221192 | tf_op jit(solution)/shard_map/ppermute | solution.py:83

commit v3 on v0

--- a/solution.py
+++ b/solution.py
@@ -44,10 +44,10 @@
         at = [elements]
         for o in range(1, A):
             at.append(move(elements, swap(o)))
-        both = [
-            jnp.stack([move(piece[0], flip(high)), move(across[1], turn(o))])
-            for o, piece in zip(range(1, R), beside)
-        ]
+        both = []
+        for o, piece in zip(range(1, R), beside):
+            one = move(piece[0], flip(high))
+            both.append(jnp.stack([one, move(across[1], turn(o))]))
         mine = jnp.concatenate([elements] + beside, axis=1)
         far = jnp.concatenate([across] + both, axis=1)
         known = {0: mine, high: far}
@@ -68,8 +68,12 @@
         at = jnp.stack(at)
         turned = [lax.dynamic_index_in_dim(at, row ^ a ^ j, 0, keepdims=False) for j in range(A)]
 
-        band_of_slot, _ = lax.optimization_barrier((band_of_slot, far))
-        slot_energy = jnp.take(energies, band_of_slot)
+        band_of_slot, energies, _ = lax.optimization_barrier((band_of_slot, energies, far))
+        if R <= 4:
+            hit = band_of_slot[None, :] == lax.iota(jnp.int32, energies.shape[0])[:, None]
+            slot_energy = jnp.sum(jnp.where(hit, energies[:, None], 0.0), axis=0)
+        else:
+            slot_energy = jnp.take(energies, band_of_slot)
         offset = slot_energy[None, :] - freq_points[:, None]
         screen = freq_weights[:, None] / (1.0 + 4.0 * offset * offset)
 

time: 53.6 us -> 50.4 us (0.940)
  local copies, waits for them, and re-layouts: 7.46 us -> 4.69 us
    gather x1 -> x0, local copies, waits for them, and re-layouts: 3.19 us -> none  [on_device(): slot_energy = jnp.take(energies, band_of_slot)]
    another operation x3, other arithmetic: 0.75 us -> 0.08 us  [on_device(): left = jnp.stack([block, jnp.stack([-block[1], block[0]])])]
    unnamed x15 -> x13, local copies, waits for them, and re-layouts: 3.72 us -> 4.13 us
  transfers between devices with their start and end apart: 12 -> 12, of which waited for: 5 -> 6; matrix products, arithmetic and copies ran while one was open for 14% -> 8% of each run, Pallas kernels for 0% -> 0%
where the time goes in v3:
time: 50.4 us; the launch traced here: 50.2 us
  waiting for transfers between devices  23.5 us (47%)
  starting transfers between devices  12.9 us (26%)
  matrix products  5.02 us (10%)
  local copies, waits for them, and re-layouts  4.69 us (9%)
  other arithmetic  3.65 us (7%)
    ppermute x12, waiting for transfers between devices, move(): return lax.ppermute(value, BOTH, pairs)  23.5 us
    ppermute x12, starting transfers between devices, move(): return lax.ppermute(value, BOTH, pairs)  12.9 us
    unnamed x13, local copies, waits for them, and re-layouts  4.13 us
    dot_general x1, matrix products, on_device(): jnp.einsum('dcmk,wcgk->wdmg', sides, screened, preferred_element_type=jnp...  3.45 us
    dot_general x4, matrix products, on_device(): jnp.einsum('dcnk,wcmk->wdnm', left, applied, preferred_element_type=jnp.f...  1.58 us
    another operation x1, other arithmetic, on_device(): at = jnp.stack(at)  1.03 us
  transfers between devices with their start and end apart: 12, of which 6 were waited for; matrix products, arithmetic and copies ran while one was open for 8% of the time, Pallas kernels for 0%

profile of v3, /device:TPU:4, one launch (start us, length us, event | category | flops | bytes accessed | tf_op | source)
XLA Modules:
  0.0 50.2 jit_solution(9695090084855673947)
XLA Ops:
  0.0 2.0 %collective-permute-start = (bf16[2,96,512]{2,1,0:T(8,128)(2,1)}, bf16[2,96,512]{2,1,0:T(8,128)(2,1)S(1)}, u32[]{:S(2)}, u32[]{:S(2)}) collective-permute-start(bf16[2,96,512]{2,1,0:T(8,128)(2,1)} %param.6), channel_id=1, source_target_pairs={{0,4},{1,5},{2,6},{3,7},{4,0},{5,1},{6,2},{7,3},{8,12},{9,13},{10,... | collective-permute-start | bytes 589832 | tf_op jit(solution)/shard_map/ppermute | solution.py:21
  2.0 3.6 %collective-permute-start.8 = (bf16[2,96,512]{2,1,0:T(8,128)(2,1)}, bf16[2,96,512]{2,1,0:T(8,128)(2,1)S(1)}, u32[]{:S(2)}, u32[]{:S(2)}) collective-permute-start(bf16[2,96,512]{2,1,0:T(8,128)(2,1)} %param.6), channel_id=1, source_target_pairs={{0,24},{1,25},{2,26},{3,27},{4,28},{5,29},{6,30},{7,31},{8,16},{9,... | collective-permute-start | bytes 589832 | tf_op jit(solution)/shard_map/ppermute | solution.py:21
  5.6 0.8 %collective-permute-start.6 = (bf16[2,96,512]{2,1,0:T(8,128)(2,1)}, bf16[2,96,512]{2,1,0:T(8,128)(2,1)S(1)}, u32[]{:S(2)}, u32[]{:S(2)}) collective-permute-start(bf16[2,96,512]{2,1,0:T(8,128)(2,1)} %param.6), channel_id=1, source_target_pairs={{0,8},{1,9},{2,10},{3,11},{4,12},{5,13},{6,14},{7,15},{8,0},{9,1},... | collective-permute-start | bytes 589832 | tf_op jit(solution)/shard_map/ppermute | solution.py:21
  6.4 1.0 %constant_dynamic-update-slice_fusion.1 = bf16[2,192,512]{2,1,0:T(8,128)(2,1)S(1)} fusion(bf16[2,96,512]{2,1,0:T(8,128)(2,1)} %param.6), kind=kLoop, calls=%fused_computation.99 | loop fusion | bytes 393216
  7.4 1.0 %collective-permute-start.4 = (bf16[96,512]{1,0:T(8,128)(2,1)S(1)}, bf16[96,512]{1,0:T(8,128)(2,1)S(1)}, u32[]{:S(2)}, u32[]{:S(2)}) collective-permute-start(bf16[96,512]{1,0:T(8,128)(2,1)S(1)} %slice_bitcast_fusion.3), channel_id=1, source_target_pairs={{0,4},{1,5},{2,6},{3,7},{4,0},{5,1},{6,2},{7,3},{8,12},{9,13},{10,... | collective-permute-start | bytes 294920 | tf_op jit(solution)/shard_map/ppermute | solution.py:21
  8.4 1.2 %collective-permute-start.3 = (bf16[96,512]{1,0:T(8,128)(2,1)S(1)}, bf16[96,512]{1,0:T(8,128)(2,1)S(1)}, u32[]{:S(2)}, u32[]{:S(2)}) collective-permute-start(bf16[96,512]{1,0:T(8,128)(2,1)S(1)} %slice_bitcast_fusion.4), channel_id=1, source_target_pairs={{0,2},{1,3},{2,0},{3,1},{4,6},{5,7},{6,4},{7,5},{8,10},{9,11},{10,... | collective-permute-start | bytes 294920 | tf_op jit(solution)/shard_map/ppermute | solution.py:21
  9.6 2.2 %collective-permute-done.8 = bf16[2,96,512]{2,1,0:T(8,128)(2,1)S(1)} collective-permute-done((bf16[2,96,512]{2,1,0:T(8,128)(2,1)}, bf16[2,96,512]{2,1,0:T(8,128)(2,1)S(1)}, u32[]{:S(2)}, u32[]{:S(2)}) %collective-permute-start.8) | collective-permute-done | bytes 196640 | tf_op jit(solution)/shard_map/ppermute | solution.py:21
  11.8 10.1 %collective-permute-done.7 = bf16[2,96,512]{2,1,0:T(8,128)(2,1)S(1)} collective-permute-done((bf16[2,96,512]{2,1,0:T(8,128)(2,1)}, bf16[2,96,512]{2,1,0:T(8,128)(2,1)S(1)}, u32[]{:S(2)}, u32[]{:S(2)}) %collective-permute-start.7) | collective-permute-done | bytes 196640 | tf_op jit(solution)/shard_map/ppermute | solution.py:21
  21.9 1.0 %pad_maximum_fusion.2 = bf16[4,2,96,512]{3,2,1,0:T(8,128)(2,1)S(1)} fusion(bf16[1,2,96,512]{3,2,1,0:T(8,128)(2,1)S(1)} %bitcast.154, bf16[1,2,96,512]{3,2,1,0:T(8,128)(2,1)S(1)} %bitcast.155, bf16[1,2,96,512]{3,2,1,0:T(8,128)(2,1)S(1)} %bitcast.156, bf16[1,2,96,512]{3,2,1,0:T(8,128)(2,1)} %bitcast.149), kind=kLoop, calls=%fused_computation.25 | loop fusion | flops 1179648 | bytes 1572864 | tf_op jit(solution)/shard_map/stack | solution.py:68
  23.0 0.1 constant_dynamic-slice_fusion.1
  23.0 0.1 fusion.35
  23.1 0.0 copy-start
  23.1 0.0 copy-start.1
  23.2 0.0 copy-start.3
  23.3 0.1 fusion.46
  23.3 0.1 collective-permute-start.5
  23.4 0.4 copy-done
  23.8 0.0 copy-done.1
  23.8 0.3 select_reduce_fusion
  24.2 0.1 fusion.40
  24.3 0.1 constant_dynamic-slice_fusion
  24.4 0.1 pad_maximum_fusion.5
  24.5 0.1 add_multiply_fusion
  24.6 0.5 collective-permute-done.5
  25.1 0.2 pad_maximum_fusion
  25.3 0.0 slice-start
  25.3 0.2 dynamic-slice_bitcast_fusion.3
  25.5 0.2 pad_maximum_fusion.1
  25.7 0.0 slice-start.1
  25.7 0.2 slice_negate_fusion
  25.9 0.3 maximum_bitcast_fusion.2
  26.2 1.3 %slice-done = s8[4194304]{0:T(1024)(128)(4,1)S(1)} async-done(((s8[8388608]{0:T(1024)(128)(4,1)}), s8[4194304]{0:T(1024)(128)(4,1)S(1)}, s32[]{:S(2)}) %slice-start) | async-done | bytes 4194328
  27.5 1.4 %slice-done.1 = s8[4194304]{0:T(1024)(128)(4,1)S(1)} async-done(((s8[8388608]{0:T(1024)(128)(4,1)}), s8[4194304]{0:T(1024)(128)(4,1)S(1)}, s32[]{:S(2)}) %slice-start.1) | async-done | bytes 4194328
  28.9 3.4 %fusion.6 = bf16[2,2,192,512,1]{3,2,0,1,4:T(8,128)(2,1)S(1)} fusion(bf16[2,2,512,2048]{3,2,1,0:T(8,128)(2,1)S(1)} %bitcast.162, bf16[1,2,192,2048]{3,2,1,0:T(8,128)(2,1)S(1)} %get-tuple-element.29, bf16[1,2,192,2048]{3,2,1,0:T(8,128)(2,1)S(1)} %get-tuple-element.28), kind=kOutput, calls=%fused_computation.12 | convolution fusion | flops 3227910144 | bytes 12320768 | tf_op jit(solution)/shard_map/dcmk,wcgk->wdmg/dot_general | solution.py:64
  32.4 0.4 fusion.14
  32.8 0.4 fusion.15
  33.2 0.2 collective-permute-start.9
  33.4 0.4 fusion.13
  33.8 1.2 %collective-permute-done.9 = f32[2,2,96,192]{2,3,1,0:T(8,128)S(1)} collective-permute-done((f32[2,2,96,192]{2,3,1,0:T(8,128)S(1)}, f32[2,2,96,192]{2,3,1,0:T(8,128)S(1)}, u32[]{:S(2)}, u32[]{:S(2)}) %collective-permute-start.9) | collective-permute-done | bytes 294944 | tf_op jit(solution)/shard_map/ppermute | solution.py:21
  35.0 1.6 %collective-permute-start.10 = (bf16[1,2,96,192]{2,3,1,0:T(8,128)(2,1)S(1)}, bf16[1,2,96,192]{2,3,1,0:T(8,128)(2,1)S(1)}, u32[]{:S(2)}, u32[]{:S(2)}) collective-permute-start(bf16[1,2,96,192]{2,3,1,0:T(8,128)(2,1)S(1)} %fusion.29), channel_id=1, source_target_pairs={{0,2},{1,3},{2,0},{3,1},{4,6},{5,7},{6,4},{7,5},{8,10},{9,11},{10,... | collective-permute-start | bytes 221192 | tf_op jit(solution)/shard_map/ppermute | solution.py:21
  36.6 0.4 fusion.16
  37.0 2.9 %collective-permute-done.10 = bf16[1,2,96,192]{2,3,1,0:T(8,128)(2,1)S(1)} collective-permute-done((bf16[1,2,96,192]{2,3,1,0:T(8,128)(2,1)S(1)}, bf16[1,2,96,192]{2,3,1,0:T(8,128)(2,1)S(1)}, u32[]{:S(2)}, u32[]{:S(2)}) %collective-permute-start.10) | collective-permute-done | bytes 73760 | tf_op jit(solution)/shard_map/ppermute | solution.py:21
  40.0 2.5 %collective-permute-start.11 = (bf16[2,96,192]{1,2,0:T(8,128)(2,1)S(1)}, bf16[2,96,192]{1,2,0:T(8,128)(2,1)S(1)}, u32[]{:S(2)}, u32[]{:S(2)}) collective-permute-start(bf16[2,96,192]{1,2,0:T(8,128)(2,1)S(1)} %fusion.32), channel_id=1, source_target_pairs={{0,0},{1,8},{2,16},{3,24},{4,4},{5,12},{6,20},{7,28},{8,1},{9,9},{... | collective-permute-start | bytes 221192 | tf_op jit(solution)/shard_map/ppermute | solution.py:21
  42.5 6.6 %collective-permute-done.11 = bf16[2,96,192]{1,2,0:T(8,128)(2,1)S(1)} collective-permute-done((bf16[2,96,192]{1,2,0:T(8,128)(2,1)S(1)}, bf16[2,96,192]{1,2,0:T(8,128)(2,1)S(1)}, u32[]{:S(2)}, u32[]{:S(2)}) %collective-permute-start.11) | collective-permute-done | bytes 73760 | tf_op jit(solution)/shard_map/ppermute | solution.py:21
  49.2 0.1 fusion.34
  49.2 0.1 copy.26
  49.3 0.1 copy.25
  49.4 0.8 %pad_maximum_fusion.4 = f32[2,96,192]{2,1,0:T(8,128)} fusion(f32[2,96,96]{2,1,0:T(8,128)S(1)} %bitcast.152, f32[2,96,96]{2,1,0:T(8,128)S(1)} %bitcast.153), kind=kLoop, calls=%fused_computation.62 | loop fusion | flops 36864 | bytes 294912 | tf_op jit(solution)/shard_map/concatenate | solution.py:106
  (24 shorter events, 0.3 us)
Async XLA Ops:
  0.0 7.4 %collective-permute-start.2 = (bf16[2,96,512]{2,1,0:T(8,128)(2,1)}, bf16[2,96,512]{2,1,0:T(8,128)(2,1)S(1)}, u32[]{:S(2)}, u32[]{:S(2)}) collective-permute-start(bf16[2,96,512]{2,1,0:T(8,128)(2,1)} %param.6), channel_id=1, source_target_pairs={{0,2},{1,3},{2,0},{3,1},{4,6},{5,7},{6,4},{7,5},{8,10},{9,11},{10,... | collective-permute-start | bytes 589832 | tf_op jit(solution)/shard_map/ppermute | solution.py:21
  0.0 8.4 %collective-permute-start = (bf16[2,96,512]{2,1,0:T(8,128)(2,1)}, bf16[2,96,512]{2,1,0:T(8,128)(2,1)S(1)}, u32[]{:S(2)}, u32[]{:S(2)}) collective-permute-start(bf16[2,96,512]{2,1,0:T(8,128)(2,1)} %param.6), channel_id=1, source_target_pairs={{0,4},{1,5},{2,6},{3,7},{4,0},{5,1},{6,2},{7,3},{8,12},{9,13},{10,... | collective-permute-start | bytes 589832 | tf_op jit(solution)/shard_map/ppermute | solution.py:21
  2.0 9.8 %collective-permute-start.8 = (bf16[2,96,512]{2,1,0:T(8,128)(2,1)}, bf16[2,96,512]{2,1,0:T(8,128)(2,1)S(1)}, u32[]{:S(2)}, u32[]{:S(2)}) collective-permute-start(bf16[2,96,512]{2,1,0:T(8,128)(2,1)} %param.6), channel_id=1, source_target_pairs={{0,24},{1,25},{2,26},{3,27},{4,28},{5,29},{6,30},{7,31},{8,16},{9,... | collective-permute-start | bytes 589832 | tf_op jit(solution)/shard_map/ppermute | solution.py:21
  5.6 16.3 %collective-permute-start.7 = (bf16[2,96,512]{2,1,0:T(8,128)(2,1)}, bf16[2,96,512]{2,1,0:T(8,128)(2,1)S(1)}, u32[]{:S(2)}, u32[]{:S(2)}) collective-permute-start(bf16[2,96,512]{2,1,0:T(8,128)(2,1)} %param.6), channel_id=1, source_target_pairs={{0,16},{1,17},{2,18},{3,19},{4,20},{5,21},{6,22},{7,23},{8,24},{9,... | collective-permute-start | bytes 589832 | tf_op jit(solution)/shard_map/ppermute | solution.py:21
  5.6 16.3 %collective-permute-start.6 = (bf16[2,96,512]{2,1,0:T(8,128)(2,1)}, bf16[2,96,512]{2,1,0:T(8,128)(2,1)S(1)}, u32[]{:S(2)}, u32[]{:S(2)}) collective-permute-start(bf16[2,96,512]{2,1,0:T(8,128)(2,1)} %param.6), channel_id=1, source_target_pairs={{0,8},{1,9},{2,10},{3,11},{4,12},{5,13},{6,14},{7,15},{8,0},{9,1},... | collective-permute-start | bytes 589832 | tf_op jit(solution)/shard_map/ppermute | solution.py:21
  7.4 15.9 %collective-permute-start.4 = (bf16[96,512]{1,0:T(8,128)(2,1)S(1)}, bf16[96,512]{1,0:T(8,128)(2,1)S(1)}, u32[]{:S(2)}, u32[]{:S(2)}) collective-permute-start(bf16[96,512]{1,0:T(8,128)(2,1)S(1)} %slice_bitcast_fusion.3), channel_id=1, source_target_pairs={{0,4},{1,5},{2,6},{3,7},{4,0},{5,1},{6,2},{7,3},{8,12},{9,13},{10,... | collective-permute-start | bytes 294920 | tf_op jit(solution)/shard_map/ppermute | solution.py:21
  8.4 14.8 %collective-permute-start.3 = (bf16[96,512]{1,0:T(8,128)(2,1)S(1)}, bf16[96,512]{1,0:T(8,128)(2,1)S(1)}, u32[]{:S(2)}, u32[]{:S(2)}) collective-permute-start(bf16[96,512]{1,0:T(8,128)(2,1)S(1)} %slice_bitcast_fusion.4), channel_id=1, source_target_pairs={{0,2},{1,3},{2,0},{3,1},{4,6},{5,7},{6,4},{7,5},{8,10},{9,11},{10,... | collective-permute-start | bytes 294920 | tf_op jit(solution)/shard_map/ppermute | solution.py:21
  11.8 12.8 %collective-permute-start.1 = (bf16[2,192,512]{2,1,0:T(8,128)(2,1)S(1)}, bf16[2,192,512]{2,1,0:T(8,128)(2,1)S(1)}, u32[]{:S(2)}, u32[]{:S(2)}) collective-permute-start(bf16[2,192,512]{2,1,0:T(8,128)(2,1)S(1)} %constant_dynamic-update-slice_fusion), channel_id=1, source_target_pairs={{0,1},{1,0},{2,3},{3,2},{4,5},{5,4},{6,7},{7,6},{8,9},{9,8},{10,11... | collective-permute-start | bytes 1179656 | tf_op jit(solution)/shard_map/ppermute | solution.py:21
  23.1 0.7 %copy-start = (f32[768]{0:T(1024)S(1)}, f32[768]{0:T(1024)}, u32[]{:S(2)}) copy-start(f32[768]{0:T(1024)} %param.8) | copy-start | bytes 9220
  23.1 0.7 %copy-start.1 = (s32[768]{0:T(1024)S(1)}, s32[768]{0:T(1024)}, u32[]{:S(2)}) copy-start(s32[768]{0:T(1024)} %param.11) | copy-start | bytes 9220
  23.1 1.0 %copy-start.2 = (f32[2]{0:T(128)S(1)}, f32[2]{0:T(128)}, u32[]{:S(2)}) copy-start(f32[2]{0:T(128)} %param.10) | copy-start | bytes 28
  23.2 1.0 %copy-start.3 = (f32[2]{0:T(128)S(1)}, f32[2]{0:T(128)}, u32[]{:S(2)}) copy-start(f32[2]{0:T(128)} %param.9) | copy-start | bytes 28
  23.3 1.8 %collective-permute-start.5 = (bf16[2,192,512]{2,1,0:T(8,128)(2,1)S(1)}, bf16[2,192,512]{2,1,0:T(8,128)(2,1)S(1)}, u32[]{:S(2)}, u32[]{:S(2)}) collective-permute-start(bf16[2,192,512]{2,1,0:T(8,128)(2,1)S(1)} %get-tuple-element.31), channel_id=1, source_target_pairs={{0,1},{1,0},{2,3},{3,2},{4,5},{5,4},{6,7},{7,6},{8,9},{9,8},{10,11... | collective-permute-start | bytes 1179656 | tf_op jit(solution)/shard_map/ppermute | solution.py:21
  25.3 2.2 %slice-start = ((s8[8388608]{0:T(1024)(128)(4,1)}), s8[4194304]{0:T(1024)(128)(4,1)S(1)}, s32[]{:S(2)}) async-start(s8[8388608]{0:T(1024)(128)(4,1)} %bitcast.161), calls=%async_computation | async-start | bytes 8388608
  25.7 3.2 %slice-start.1 = ((s8[8388608]{0:T(1024)(128)(4,1)}), s8[4194304]{0:T(1024)(128)(4,1)S(1)}, s32[]{:S(2)}) async-start(s8[8388608]{0:T(1024)(128)(4,1)} %bitcast.161), calls=%async_computation.1 | async-start | bytes 8388608
  33.2 1.8 %collective-permute-start.9 = (f32[2,2,96,192]{2,3,1,0:T(8,128)S(1)}, f32[2,2,96,192]{2,3,1,0:T(8,128)S(1)}, u32[]{:S(2)}, u32[]{:S(2)}) collective-permute-start(f32[2,2,96,192]{2,3,1,0:T(8,128)S(1)} %pad_maximum_fusion.3), channel_id=1, source_target_pairs={{0,1},{1,0},{2,3},{3,2},{4,5},{5,4},{6,7},{7,6},{8,9},{9,8},{10,11... | collective-permute-start | bytes 884744 | tf_op jit(solution)/shard_map/ppermute | solution.py:21
  35.0 4.9 %collective-permute-start.10 = (bf16[1,2,96,192]{2,3,1,0:T(8,128)(2,1)S(1)}, bf16[1,2,96,192]{2,3,1,0:T(8,128)(2,1)S(1)}, u32[]{:S(2)}, u32[]{:S(2)}) collective-permute-start(bf16[1,2,96,192]{2,3,1,0:T(8,128)(2,1)S(1)} %fusion.29), channel_id=1, source_target_pairs={{0,2},{1,3},{2,0},{3,1},{4,6},{5,7},{6,4},{7,5},{8,10},{9,11},{10,... | collective-permute-start | bytes 221192 | tf_op jit(solution)/shard_map/ppermute | solution.py:21
  40.0 9.2 %collective-permute-start.11 = (bf16[2,96,192]{1,2,0:T(8,128)(2,1)S(1)}, bf16[2,96,192]{1,2,0:T(8,128)(2,1)S(1)}, u32[]{:S(2)}, u32[]{:S(2)}) collective-permute-start(bf16[2,96,192]{1,2,0:T(8,128)(2,1)S(1)} %fusion.32), channel_id=1, source_target_pairs={{0,0},{1,8},{2,16},{3,24},{4,4},{5,12},{6,20},{7,28},{8,1},{9,9},{... | collective-permute-start | bytes 221192 | tf_op jit(solution)/shard_map/ppermute | solution.py:21
